TPU v7x, 32 devices: a whole 2x2x4 slice. The times are simulated.
32 devices in a mesh: gx: 4 (over x, core), gy: 2 (over y), gz: 4 (over z).
Axes of the slice: x: 2, y: 2, z: 4, core: 2. Of those that a mesh axis runs over, the one named last changes fastest.
Arguments:
- right_side: float32 [32, 32, 512], P('gx', 'gy', 'gz'), may hold values from -6 to 6
- conductance: float32 [32, 32, 512], P('gx', 'gy', 'gz'), may hold values from 0.25 to 4
- extents: int32 [4, 2, 4], P('gx', 'gy', 'gz'), may hold values from 64 to 128, as said below
- coarse_factor: bfloat16 [32, 32], replicated, may hold values from -1 to 3, as said below
Outputs:
- solution_field: float32 [32, 32, 512], P('gx', 'gy', 'gz')
- residual: float32 [32, 32, 512], P('gx', 'gy', 'gz')
Inputs may be any that keep to these rules, and one draw needn't show every extreme that they name: `extents`: cells of a block whose third local index is below its count are fluid, the others padding; in every draw some block has all 128 layers fluid. `coarse_factor`: lower triangular with a positive diagonal.
All inputs are finite; a program needn't handle non-finite values.
Results may differ from a plain program's by a relative error of at most 0.0003.
Values sent between devices are 32-bit elements; how exact they have to be, the bound alone decides.
A program may use at most 64 MiB of HBM per device.

v0:
```python
import functools

import jax
import jax.numpy as jnp
from jax import lax
from jax.experimental import pallas as pl
from jax.experimental.pallas import tpu as pltpu
from jax.sharding import PartitionSpec as P

OMEGA = 0.8
HALO = 4
MESH = pl.DeviceIdType.MESH
HIGH = lax.Precision.HIGHEST
DIRS = [
    (dx, dy, dz)
    for dx in (-1, 0, 1)
    for dy in (-1, 0, 1)
    for dz in (-1, 0, 1)
    if (dx, dy, dz) != (0, 0, 0)
]
DIRS.sort(key=lambda d: -sum(abs(a) for a in d))


def code(dx, dy, dz):
    return (dx + 1) * 9 + (dy + 1) * 3 + dz + 1


def kernel(
    counts,
    rhs_hbm,
    cond_hbm,
    ext_ref,
    factor_hbm,
    sol_ref,
    res_ref,
    rhs_ref,
    cond_ref,
    factor_ref,
    h_out,
    p_out,
    e_out,
    x_in,
    h_in,
    p_in,
    e_in,
    av_out,
    h2_out,
    p2_out,
    x2_in,
    h2_in,
    p2_in,
    row_out,
    row2_out,
    gath,
    gath2,
    R,
    C,
    FL,
    FX,
    FY,
    FZ,
    INV,
    C1,
    IC,
    FIRST,
    SEC,
    V,
    U,
    YT,
    D0,
    AD0,
    AV1,
    send_a,
    recv_a,
    send_e,
    recv_e,
    send_b,
    recv_b,
    send_g,
    recv_g,
    load_sem,
):
    ngx, ngy, ngz = counts
    n = ngx * ngy * ngz
    ix, iy, iz = lax.axis_index("gx"), lax.axis_index("gy"), lax.axis_index("gz")
    me = (ix * ngy + iy) * ngz + iz
    bx, by, bz = rhs_ref.shape
    ex, ey, ez = bx + 2 * HALO, by + 2 * HALO, 2 * bz
    group = 2 * HALO
    half = bz // 2
    f32 = jnp.float32

    loads = [
        pltpu.make_async_copy(src, dst, load_sem.at[k])
        for k, (src, dst) in enumerate(
            ((rhs_hbm, rhs_ref), (cond_hbm, cond_ref), (factor_hbm, factor_ref))
        )
    ]
    for load in loads:
        load.start()

    def turned(at, step, count):
        moved = at + step
        return jnp.where(moved >= count, moved - count, moved)

    def everyone(act):
        if n <= 64:
            xs = [turned(ix, t, ngx) for t in range(ngx)]
            ys = [turned(iy, t, ngy) for t in range(ngy)]
            zs = [turned(iz, t, ngz) for t in range(ngz)]
            steps = [(a, b, c) for a in range(ngx) for b in range(ngy) for c in range(ngz)]
            steps.sort(
                key=lambda t: -sum(min(a, m - a) for a, m in zip(t, (ngx, ngy, ngz)))
            )
            for a, b, c in steps[:-1]:
                act((xs[a], ys[b], zs[c]))
        else:

            def one(t, carry):
                flat = (me + t) % n
                act((flat // (ngy * ngz), (flat // ngz) % ngy, flat % ngz))
                return carry

            lax.fori_loop(1, n, one, 0)

    for buf in (x_in, h_in, p_in, e_in, x2_in, h2_in, p2_in):
        buf[...] = jnp.zeros(buf.shape, f32)

    barrier = pltpu.get_barrier_semaphore()
    everyone(
        lambda device: pl.semaphore_signal(
            barrier, inc=1, device_id=device, device_id_type=MESH
        )
    )

    lane = lax.broadcasted_iota(jnp.int32, (ey, bz), 1)
    row8 = lax.broadcasted_iota(jnp.int32, (2 * HALO, bz), 0)

    def edge_tile(slab):
        return jnp.where(row8 < HALO, slab[: 2 * HALO], slab[by - 2 * HALO :])

    def pack_pairs(out, lows, highs):
        for p in range(len(lows) // 2):
            out[0][p] = jnp.where(
                row8 < HALO, pltpu.roll(highs[2 * p], HALO, 0), highs[2 * p + 1]
            )
            out[1][p] = jnp.where(
                row8 < HALO, lows[2 * p], pltpu.roll(lows[2 * p + 1], HALO, 0)
            )

    def pack(slabs):
        packed = jnp.zeros((ey, bz), f32)
        for at, (slab, tile) in enumerate(slabs):
            full = jnp.concatenate([slab, tile], axis=0)
            moved = pltpu.roll(full, (HALO + group * at) % bz, 1)
            packed = jnp.where(lane // group == at, moved, packed)
        return packed

    for load in loads[:2]:
        load.wait()
    tall = 2 * HALO
    slabs = []
    for f, ref in enumerate((rhs_ref, cond_ref)):
        fields = [ref[x] for x in range(bx)]
        pack_pairs(
            (h_out.at[0, f], h_out.at[1, f]),
            [v[:tall] for v in fields],
            [v[by - tall :] for v in fields],
        )
        slabs.extend((v, edge_tile(v)) for v in fields)
    p_out[...] = pack(slabs)
    own_limit = ext_ref[0, 0, 0]
    e_out[...] = jnp.full((1, bz), own_limit.astype(f32), f32)

    pl.semaphore_wait(barrier, n - 1)

    def inside(d):
        dx, dy, dz = d
        ok = None
        for at, step, count in ((ix, dx, ngx), (iy, dy, ngy), (iz, dz, ngz)):
            if step == 0:
                continue
            here = (at + step >= 0) & (at + step < count)
            ok = here if ok is None else ok & here
        return ok

    def target(d):
        return (ix + d[0], iy + d[1], iz + d[2])

    def remote(src, dst, send, recv, d):
        return pltpu.make_async_remote_copy(
            src_ref=src,
            dst_ref=dst,
            send_sem=send,
            recv_sem=recv,
            device_id=target(d),
            device_id_type=MESH,
        )

    def x_part(dx):
        return pl.ds(bx - HALO, HALO) if dx == 1 else pl.ds(0, HALO)

    def pair_part(dx):
        few, all_ = HALO // 2, bx // 2
        if dx == 0:
            return pl.ds(0, all_), pl.ds(few, all_)
        if dx == 1:
            return pl.ds(all_ - few, few), pl.ds(0, few)
        return pl.ds(0, few), pl.ds(all_ + few, few)

    def p_rows(dy):
        return pl.ds(0, by) if dy == 0 else pl.ds(by, tall)

    def side(dx):
        return 0 if dx == 1 else 1

    def copies_a(d):
        dx, dy, dz = d
        k = code(*d)
        out = [remote(e_out, e_in.at[code(-dx, -dy, -dz)], send_e.at[k], recv_e.at[k], d)]
        if dz != 0:
            slot = code(-dx, -dy, -dz)
            rows = p_rows(dy)
            out.append(
                remote(
                    p_out.at[rows], p_in.at[slot, rows], send_a.at[k, 0], recv_a.at[k, 0], d
                )
            )
        elif dy != 0:
            src, dst = pair_part(dx)
            out.append(
                remote(
                    h_out.at[side(dy), :, src],
                    h_in.at[side(dy), :, dst],
                    send_a.at[k, 0],
                    recv_a.at[k, 0],
                    d,
                )
            )
        else:
            src = x_part(dx)
            for f, ref in enumerate((rhs_ref, cond_ref)):
                out.append(
                    remote(
                        ref.at[src],
                        x_in.at[side(dx), f],
                        send_a.at[k, f],
                        recv_a.at[k, f],
                        d,
                    )
                )
        return out

    def copies_b(d):
        dx, dy, dz = d
        k = code(*d)
        if dz != 0:
            slot = code(-dx, -dy, -dz)
            rows = p_rows(dy)
            return [
                remote(p2_out.at[rows], p2_in.at[slot, rows], send_b.at[k], recv_b.at[k], d)
            ]
        if dy != 0:
            src, dst = pair_part(dx)
            return [
                remote(
                    h2_out.at[side(dy), src], h2_in.at[side(dy), dst], send_b.at[k], recv_b.at[k], d
                )
            ]
        src = x_part(dx)
        return [remote(av_out.at[src], x2_in.at[side(dx)], send_b.at[k], recv_b.at[k], d)]

    def start_all(copies):
        for d in DIRS:

            @pl.when(inside(d))
            def _():
                for c in copies(d):
                    c.start()

    def wait_all(copies):
        for d in DIRS:
            @pl.when(inside(tuple(-a for a in d)))
            def _():
                for c in copies(d):
                    c.wait_recv()

    def wait_sent(copies):
        for d in DIRS:

            @pl.when(inside(d))
            def _():
                for c in copies(d):
                    c.wait_send()

    start_all(copies_a)

    loads[2].wait()
    L = factor_ref[...].astype(f32)
    ri = lax.broadcasted_iota(jnp.int32, (n, n), 0)
    ci = lax.broadcasted_iota(jnp.int32, (n, n), 1)
    eye = ri == ci
    X = jnp.where(eye, 1.0 / jnp.where(eye, L, 1.0), 0.0)
    s = 1
    while s < n:
        pick = (ri // (2 * s) == ci // (2 * s)) & (ri % (2 * s) >= s) & (ci % (2 * s) < s)
        low = jnp.where(pick, L, 0.0)
        X = X - jnp.dot(
            X,
            jnp.dot(low, X, precision=HIGH, preferred_element_type=f32),
            precision=HIGH,
            preferred_element_type=f32,
        )
        s *= 2
    W = lax.dot_general(
        X, X, (((0,), (0,)), ((), ())), precision=HIGH, preferred_element_type=f32
    )

    rowe = lax.broadcasted_iota(jnp.int32, (ey, bz), 0)
    low_lanes = (lane % group) < HALO

    def merge_h(h, x, *at):
        low, high = h[(0,) + at + (x // 2,)], h[(1,) + at + (x // 2,)]
        if x % 2 == 0:
            return jnp.where(row8 < HALO, high, pltpu.roll(low, HALO, 0))
        return jnp.where(row8 < HALO, pltpu.roll(high, HALO, 0), low)

    def merge_p(p):
        merged = []
        for dx in (-1, 0, 1):

            def from_z(dy):
                return jnp.where(
                    low_lanes, p[code(dx, dy, 1)], p[code(dx, dy, -1)]
                ), jnp.where(low_lanes, p[code(dx, dy, -1)], p[code(dx, dy, 1)])

            mid = from_z(0)[1]
            up = from_z(1)[1]
            down = from_z(-1)[1]
            merged.append(
                jnp.where(rowe < by, mid, jnp.where(rowe < by + HALO, up, down))
            )
        return merged

    def where_from(x):
        if x < HALO:
            return 0, bx - HALO + x
        if x < HALO + bx:
            return 1, x - HALO
        return 2, x - HALO - bx

    def unpack(merged, x, f):
        which, slab = where_from(x)
        at = f * bx + slab
        return pltpu.roll(merged[which], (bz - HALO - group * at) % bz, 1)

    wait_all(copies_a)

    merged = merge_p(p_in)
    limits = []
    for dx in (-1, 0, 1):
        sides = []
        for dz in (0, 1, -1):

            def limit(dy):
                if (dx, dy, dz) == (0, 0, 0):
                    return e_out[...]
                return e_in[code(dx, dy, dz)]

            sides.append(
                jnp.where(rowe < by, limit(0), jnp.where(rowe < by + HALO, limit(1), limit(-1)))
            )
        limits.append((sides[0], jnp.where(lane < half, sides[1], sides[2])))
    flags, flags1 = [], []
    lane_f = lane.astype(f32)
    even_f = (lane - lane % 2).astype(f32)
    for a, b in limits:
        flags.append(
            jnp.concatenate([(lane_f < a).astype(f32), (lane_f < b).astype(f32)], axis=1)
        )
        flags1.append(
            jnp.concatenate([(even_f < a).astype(f32), (even_f < b).astype(f32)], axis=1)
        )
    for x in range(ex):
        which, _ = where_from(x)
        FL[x] = flags[which]
        for f, (ref, field) in enumerate(((rhs_ref, R), (cond_ref, C))):
            if which == 1:
                core = ref[x - HALO]
            elif which == 0:
                core = x_in[0, f, x]
            else:
                core = x_in[1, f, x - HALO - bx]
            a = jnp.concatenate([core, merge_h(h_in, x, f)], axis=0)
            whole = jnp.concatenate([a, unpack(merged, x, f)], axis=1)
            field[x] = whole * flags[which] if f == 0 else whole

    wide_lane = lax.broadcasted_iota(jnp.int32, (ey, ez), 1)
    wide_row = lax.broadcasted_iota(jnp.int32, (ey, ez), 0)
    odd_lane = wide_lane % 2 == 1
    odd_row = wide_row % 2 == 1

    def up_y(v, k=1):
        return pltpu.roll(v, k, 0)

    def dn_y(v, k=1):
        return pltpu.roll(v, ey - k, 0)

    def up_z(v, k=1):
        return pltpu.roll(v, k, 1)

    def dn_z(v, k=1):
        return pltpu.roll(v, ez - k, 1)

    def pool_yz(v):
        v = v + jnp.where(odd_row, up_y(v), dn_y(v))
        return v + jnp.where(odd_lane, up_z(v), dn_z(v))

    for x in range(ex):
        c = C[x]
        if x > 0:
            FX[x] = 0.5 * (C[x - 1] + c)
        FY[x] = 0.5 * (c + up_y(c))
        FZ[x] = 0.5 * (c + up_z(c))
    for x in range(1, ex - 1):
        fy, fz = FY[x], FZ[x]
        total = FX[x] + FX[x + 1] + fy + dn_y(fy) + fz + dn_z(fz)
        fl = FL[x]
        INV[x] = OMEGA * fl / (total + 1.0 - fl)
    for q in range(ex // 2):
        C1[q] = pool_yz(C[2 * q] + C[2 * q + 1]) * 0.125
    for q in range(1, ex // 2 - 1):
        c = C1[q]
        total = 3.0 * c + 0.5 * (
            C1[q - 1] + C1[q + 1] + up_y(c, 2) + dn_y(c, 2) + up_z(c, 2) + dn_z(c, 2)
        )
        fl = flags1[where_from(2 * q)[0]]
        IC[q] = OMEGA * fl / (4.0 * total + 1.0 - fl)

    def apply(src, x):
        v = src[x]
        gx = FX[x] * (v - src[x - 1]) + FX[x + 1] * (v - src[x + 1])
        gy = FY[x] * (v - up_y(v))
        gz = FZ[x] * (v - up_z(v))
        return FL[x] * (gx + (gy - dn_y(gy)) + (gz - dn_z(gz)))

    def core(v):
        return v[:by, :bz]

    def cycle():
        for x in range(1, ex - 1):
            FIRST[x] = INV[x] * R[x]
        for q in range(1, ex // 2 - 1):
            a, b = 2 * q, 2 * q + 1
            gap = (R[a] - apply(FIRST, a)) + (R[b] - apply(FIRST, b))
            below = IC[q] * pool_yz(gap)
            SEC[a] = FIRST[a] + FL[a] * below
            SEC[b] = FIRST[b] + FL[b] * below
        for x in range(3, ex - 3):
            V[x] = SEC[x] + INV[x] * (R[x] - apply(SEC, x))

    def total(v):
        return jnp.sum(v, axis=(0, 1), keepdims=True)

    width = gath.shape[-1]
    col = lax.broadcasted_iota(jnp.int32, (1, width), 1)

    def spread(row_ref, g, base):
        everyone(lambda device: remote_row(row_ref, g, base, device).start())

    def remote_row(row_ref, g, base, device):
        return pltpu.make_async_remote_copy(
            src_ref=row_ref,
            dst_ref=g.at[me],
            send_sem=send_g.at[base],
            recv_sem=recv_g.at[base],
            device_id=device,
            device_id_type=MESH,
        )

    def collect(g, base):
        part = g.at[pl.ds(0, n - 1)]
        pltpu.make_async_copy(part, part, recv_g.at[base]).wait()
        pltpu.make_async_copy(part, part, send_g.at[base]).wait()

    cells = bx * by * bz

    cycle()
    sums = [jnp.zeros((by, bz), f32) for _ in range(4)]
    slabs = []
    for x in range(bx):
        e = x + HALO
        av = core(apply(V, e))
        v, r = core(V[e]), core(R[e])
        av_out[x] = av
        slabs.append((av, edge_tile(av)))
        sums = [sums[0] + r, sums[1] + r * v, sums[2] + v * av, sums[3] + av]
    pack_pairs(
        (h2_out.at[0], h2_out.at[1]),
        [v[:tall] for v, _ in slabs],
        [v[by - tall :] for v, _ in slabs],
    )
    p2_out[...] = pack(slabs)
    start_all(copies_b)

    acc = jnp.zeros((by, bz), f32)
    for x in range(HALO, HALO + bx):
        acc = acc + core(apply(FL, x))
    faces = []
    for dx, x, near in ((-1, HALO, HALO - 1), (1, HALO + bx, HALO + bx - 1)):
        other = FL[x] if dx == 1 else FL[near]
        mine = FL[near] if dx == 1 else FL[x]
        faces.append(((dx, 0, 0), total(core(FX[x] * mine * other))))
    first_row = wide_row[:by, :bz] == 0
    last_row = wide_row[:by, :bz] == by - 1
    first_lane = wide_lane[:by, :bz] == 0
    last_lane = wide_lane[:by, :bz] == bz - 1
    cy = jnp.zeros((ey, ez), f32)
    cz = jnp.zeros((ey, ez), f32)
    for x in range(HALO, HALO + bx):
        fl = FL[x]
        cy = cy + FY[x] * fl * up_y(fl)
        cz = cz + FZ[x] * fl * up_z(fl)
    cy_hi, cz_hi = core(dn_y(cy)), core(dn_z(cz))
    faces.append(((0, -1, 0), total(jnp.where(first_row, core(cy), 0.0))))
    faces.append(((0, 1, 0), total(jnp.where(last_row, cy_hi, 0.0))))
    faces.append(((0, 0, -1), total(jnp.where(first_lane, core(cz), 0.0))))
    faces.append(((0, 0, 1), total(jnp.where(last_lane, cz_hi, 0.0))))
    diagonal = total(acc)
    row = jnp.zeros((1, width), f32)
    for (dx, dy, dz), g in faces:
        diagonal = diagonal + g
        other = ((ix + dx) * ngy + iy + dy) * ngz + iz + dz
        row = row - jnp.where(col == bz + other, g, 0.0)
    row = row + jnp.where(col == bz + me, diagonal, 0.0)
    for k, part in enumerate(sums):
        row = jnp.where(col == k, total(part), row)
    row_out[...] = row
    gath[pl.ds(me, 1)] = row[None]
    spread(row_out, gath, 0)
    collect(gath, 0)

    def column(g, k):
        return g[:, 0, k : k + 1]

    def solve(means_col):
        y_row = jnp.sum(W * means_col, axis=0, keepdims=True)
        y_col = jnp.sum(jnp.where(eye, y_row, 0.0), axis=1, keepdims=True)
        return y_row, y_col

    ycol_id = lax.broadcasted_iota(jnp.int32, (ey, n), 1)
    yrow_id = lax.broadcasted_iota(jnp.int32, (ey, n), 0)
    dy_id = jnp.where(yrow_id < by, 0, jnp.where(yrow_id < by + HALO, 1, -1))

    def make_table(y_row):
        for dx in (-1, 0, 1):
            cols = []
            for dz in (0, 1, -1):
                where_at = ((ix + dx) * ngy + iy + dy_id) * ngz + iz + dz
                cols.append(
                    jnp.sum(jnp.where(ycol_id == where_at, y_row, 0.0), axis=1, keepdims=True)
                )
            YT[dx + 1] = jnp.concatenate(
                [
                    jnp.broadcast_to(cols[0], (ey, bz)),
                    jnp.where(lane < half, cols[1], cols[2]),
                ],
                axis=1,
            )

    coupling = gath[:, 0, bz : bz + n]
    m0 = column(gath, 0)
    y_row, y_col = solve(m0 * (1.0 / cells))
    rz = total(column(gath, 1)) + total(m0 * y_col)
    dad = (
        total(column(gath, 2))
        + 2.0 * total(column(gath, 3) * y_col)
        + total(coupling * y_col * y_row)
    )
    alpha = rz / dad
    make_table(y_row)
    for x in range(ex):
        U[x] = FL[x] * YT[where_from(x)[0]]

    wait_all(copies_b)
    merged = merge_p(p2_in)
    for x in range(1, ex - 1):
        which, _ = where_from(x)
        au = apply(U, x)
        if which == 1:
            mid = av_out[x - HALO]
        elif which == 0:
            mid = x2_in[0, x]
        else:
            mid = x2_in[1, x - HALO - bx]
        a = jnp.concatenate([mid, merge_h(h2_in, x)], axis=0)
        ad = jnp.concatenate([a, unpack(merged, x, 0)], axis=1) + au
        R[x] = R[x] - alpha * ad
        if which == 1:
            AD0[x - HALO] = core(ad)
            D0[x - HALO] = core(V[x]) + core(U[x])

    cycle()
    sums = [jnp.zeros((by, bz), f32) for _ in range(6)]
    for x in range(bx):
        e = x + HALO
        av = core(apply(V, e))
        v, r, ad0 = core(V[e]), core(R[e]), AD0[x]
        AV1[x] = av
        sums = [
            sums[0] + r,
            sums[1] + r * v,
            sums[2] + v * av,
            sums[3] + av,
            sums[4] + v * ad0,
            sums[5] + ad0,
        ]
    row = jnp.zeros((1, bz), f32)
    for k, part in enumerate(sums):
        row = jnp.where(col[:, :bz] == k, total(part), row)
    row2_out[...] = row
    gath2[pl.ds(me, 1)] = row[None]
    spread(row2_out, gath2, 1)
    collect(gath2, 1)
    m1 = column(gath2, 0)
    y_row, y_col = solve(m1 * (1.0 / cells))
    new = total(column(gath2, 1)) + total(m1 * y_col)
    beta = new / rz
    dad1 = (
        total(column(gath2, 2))
        + 2.0 * total(column(gath2, 3) * y_col)
        + total(coupling * y_col * y_row)
        + 2.0 * beta * (total(column(gath2, 4)) + total(column(gath2, 5) * y_col))
        + beta * beta * dad
    )
    alpha1 = new / dad1
    make_table(y_row)
    for x in range(HALO - 1, HALO + bx + 1):
        U[x] = FL[x] * YT[where_from(x)[0]]
    for x in range(bx):
        e = x + HALO
        d1 = core(V[e]) + core(U[e]) + beta * D0[x]
        ad1 = AV1[x] + core(apply(U, e)) + beta * AD0[x]
        sol_ref[x] = alpha * D0[x] + alpha1 * d1
        res_ref[x] = core(R[e]) - alpha1 * ad1
    wait_sent(copies_a)
    wait_sent(copies_b)


def solution(mesh):
    counts = (mesh.shape["gx"], mesh.shape["gy"], mesh.shape["gz"])
    n = counts[0] * counts[1] * counts[2]

    def on_device(right_side, conductance, extents, coarse_factor):
        f32 = jnp.float32
        bx, by, bz = right_side.shape
        ex, ey, ez = bx + 2 * HALO, by + 2 * HALO, 2 * bz
        tall = 2 * HALO
        width = bz + -(-n // 128) * 128
        vm = lambda *shape: pltpu.VMEM(shape, f32)
        field = vm(ex, ey, ez)
        dma = pltpu.SemaphoreType.DMA
        scratch = [
            vm(bx, by, bz),
            vm(bx, by, bz),
            pltpu.VMEM(coarse_factor.shape, coarse_factor.dtype),
            vm(2, 2, bx // 2, tall, bz),
            vm(ey, bz),
            vm(1, bz),
            vm(2, 2, HALO, by, bz),
            vm(2, 2, ex // 2, tall, bz),
            vm(27, ey, bz),
            vm(27, 1, bz),
            vm(bx, by, bz),
            vm(2, bx // 2, tall, bz),
            vm(ey, bz),
            vm(2, HALO, by, bz),
            vm(2, ex // 2, tall, bz),
            vm(27, ey, bz),
            vm(1, width),
            vm(1, bz),
            vm(n, 1, width),
            vm(n, 1, bz),
            field,
            field,
            field,
            field,
            field,
            field,
            field,
            vm(ex // 2, ey, ez),
            vm(ex // 2, ey, ez),
            field,
            field,
            field,
            field,
            vm(3, ey, ez),
            vm(bx, by, bz),
            vm(bx, by, bz),
            vm(bx, by, bz),
            dma((27, 2)),
            dma((27, 2)),
            dma((27,)),
            dma((27,)),
            dma((27,)),
            dma((27,)),
            dma((2,)),
            dma((2,)),
            dma((3,)),
        ]
        block = vm(bx, by, bz)
        whole = pl.BlockSpec(memory_space=pltpu.VMEM)
        outer = pl.BlockSpec(memory_space=pltpu.HBM)
        return pl.pallas_call(
            functools.partial(kernel, counts),
            out_shape=(block, block),
            in_specs=[outer, outer, pl.BlockSpec(memory_space=pltpu.SMEM), outer],
            out_specs=(whole, whole),
            scratch_shapes=scratch,
            compiler_params=pltpu.CompilerParams(
                collective_id=0, has_side_effects=True, vmem_limit_bytes=60000000
            ),
        )(right_side, conductance, extents, coarse_factor)

    in_specs = (P("gx", "gy", "gz"), P("gx", "gy", "gz"), P("gx", "gy", "gz"), P())
    out_specs = (P("gx", "gy", "gz"), P("gx", "gy", "gz"))
    return jax.shard_map(
        on_device, mesh=mesh, in_specs=in_specs, out_specs=out_specs, check_vma=False
    )
```

profile of v0, /device:TPU:0, one launch (start us, length us, event | category | flops | bytes accessed | tf_op | source)
XLA Modules:
  0.0 27.4 jit_solution(9182481158106327158)
XLA Ops:
  1.3 24.9 %shard_map.59 = (f32[8,16,128]{2,1,0:T(8,128)S(1)}, f32[8,16,128]{2,1,0:T(8,128)S(1)}) custom-call(f32[8,16,128]{2,1,0:T(8,128)} %rhs_hbm.1, f32[8,16,128]{2,1,0:T(8,128)} %cond_hbm.1, s32[1,1,1]{2,1,0:T(1,128)S(6)} %copy.10.ext_ref, bf16[32,32]{1,0:T(8,128)(2,1)} %factor_hbm.1), custom_call_target="tpu_custom_call" | custom-call | tf_op jit(solution)/shard_map/pallas_call | solution.py:714
  26.2 0.6 %copy.8 = f32[8,16,128]{2,1,0:T(8,128)} copy(f32[8,16,128]{2,1,0:T(8,128)S(1)} %get-tuple-element.2) | data formatting | bytes 131072
  26.8 0.6 %copy.9 = f32[8,16,128]{2,1,0:T(8,128)} copy(f32[8,16,128]{2,1,0:T(8,128)S(1)} %get-tuple-element.3) | data formatting | bytes 131072
where the time goes:
time: 27.6 us; the launch traced here: 27.4 us
  Pallas kernels  24.9 us (90%)
  between operations  1.28 us (5%)
  local copies, waits for them, and re-layouts  1.26 us (5%)
    pallas_call x1, Pallas kernels, on_device(): pl.pallas_call(functools.partial(kernel, counts), out_shape=(block, block...  24.9 us
    unnamed x2, local copies, waits for them, and re-layouts  1.26 us

commit v1 on v0

v1 whole, which is shorter than its diff:
```python
import functools

import jax
import jax.numpy as jnp
from jax import lax
from jax.experimental import pallas as pl
from jax.experimental.pallas import tpu as pltpu
from jax.sharding import PartitionSpec as P

OMEGA = 0.8
HALO = 8
GROUP = 3 * HALO
MESH = pl.DeviceIdType.MESH
HIGH = lax.Precision.HIGHEST
DIRS = [
    (dx, dy, dz)
    for dx in (-1, 0, 1)
    for dy in (-1, 0, 1)
    for dz in (-1, 0, 1)
    if (dx, dy, dz) != (0, 0, 0)
]
DIRS.sort(key=lambda d: -sum(abs(a) for a in d))


def code(dx, dy, dz):
    return (dx + 1) * 9 + (dy + 1) * 3 + dz + 1


class Edge:
    def __init__(self, bx, bz):
        self.bx, self.ex = bx, bx + 2 * HALO
        self.places = bz // GROUP
        tiles = -(-2 * self.ex // self.places)
        self.tiles = tiles + tiles % 2
        self.patterns, self.pattern_of = [], []
        for t in range(self.tiles):
            key = tuple(
                None if s is None else (self.block(s[0])[0], s[1])
                for s in (self.slab(t, j) for j in range(self.places))
            )
            if key not in self.patterns:
                self.patterns.append(key)
            self.pattern_of.append(self.patterns.index(key))

    def slab(self, t, j):
        slot = t + self.tiles * j
        return None if slot >= 2 * self.ex else (slot % self.ex, slot // self.ex)

    def place(self, s, side):
        slot = s + self.ex * side
        return slot % self.tiles, slot // self.tiles

    def block(self, s):
        if s < HALO:
            return 0, self.bx - HALO + s
        if s < HALO + self.bx:
            return 1, s - HALO
        return 2, s - HALO - self.bx


def kernel(
    counts,
    rhs_hbm,
    cond_hbm,
    ext_hbm,
    factor_hbm,
    sol_ref,
    res_ref,
    R,
    C,
    ext_ref,
    factor_ref,
    e_out,
    e_in,
    z_out,
    z_in,
    early_out,
    early,
    late_out,
    late,
    FL,
    F1,
    FX,
    FY,
    FZ,
    INV,
    C1,
    IC,
    SEC,
    D0,
    W,
    U,
    Q,
    YB,
    EY,
    send_c,
    recv_c,
    send_r,
    recv_r,
    send_e,
    recv_e,
    send_g,
    recv_g,
    load_sem,
):
    ngx, ngy, ngz = counts
    n = ngx * ngy * ngz
    ix, iy, iz = lax.axis_index("gx"), lax.axis_index("gy"), lax.axis_index("gz")
    me = (ix * ngy + iy) * ngz + iz
    bx, by, bz = sol_ref.shape
    ex, ey = bx + 2 * HALO, by + 2 * HALO
    edge = Edge(bx, bz)
    tiles = edge.tiles
    f32 = jnp.float32
    lo_x, hi_x = HALO, HALO + bx

    def turned(at, step, count):
        moved = at + step
        return jnp.where(moved >= count, moved - count, moved)

    def everyone(act):
        if n <= 64:
            xs = [turned(ix, t, ngx) for t in range(ngx)]
            ys = [turned(iy, t, ngy) for t in range(ngy)]
            zs = [turned(iz, t, ngz) for t in range(ngz)]
            steps = [(a, b, c) for a in range(ngx) for b in range(ngy) for c in range(ngz)]
            steps.sort(
                key=lambda t: -sum(min(a, m - a) for a, m in zip(t, (ngx, ngy, ngz)))
            )
            for a, b, c in steps[:-1]:
                act((xs[a], ys[b], zs[c]))
        else:

            def one(t, carry):
                flat = (me + t) % n
                act((flat // (ngy * ngz), (flat // ngz) % ngy, flat % ngz))
                return carry

            lax.fori_loop(1, n, one, 0)

    core_x, core_y = pl.ds(lo_x, bx), pl.ds(0, by)
    loads = [
        pltpu.make_async_copy(src, dst, load_sem.at[k])
        for k, (src, dst) in enumerate(
            (
                (rhs_hbm, R.at[core_x, core_y]),
                (cond_hbm, C.at[core_x, core_y]),
                (ext_hbm, ext_ref),
                (factor_hbm, factor_ref),
            )
        )
    ]
    for load in loads:
        load.start()

    barrier = pltpu.get_barrier_semaphore()
    everyone(
        lambda device: pl.semaphore_signal(
            barrier, inc=1, device_id=device, device_id_type=MESH
        )
    )

    def inside(d):
        ok = None
        for at, step, count in zip((ix, iy, iz), d, counts):
            if step == 0:
                continue
            here = (at + step >= 0) & (at + step < count)
            ok = here if ok is None else ok & here
        return ok

    def x_from(dx):
        return pl.ds(bx, HALO) if dx == 1 else pl.ds(HALO, bx if dx == 0 else HALO)

    def x_into(dx):
        if dx == 0:
            return pl.ds(HALO, bx)
        return pl.ds(0, HALO) if dx == 1 else pl.ds(hi_x, HALO)

    def y_from(dy):
        return pl.ds(by - HALO, HALO) if dy == 1 else pl.ds(0, by if dy == 0 else HALO)

    def y_into(dy):
        if dy == 0:
            return pl.ds(0, by)
        return pl.ds(by + HALO, HALO) if dy == 1 else pl.ds(by, HALO)

    def landing(f, d):
        dx, dy, dz = d
        if dz != 0:
            return z_in.at[f, 1 if dz == 1 else 0, 1 - dx, y_into(dy)]
        return (R, C)[f].at[x_into(dx), y_into(dy)]

    def remote(src, dst, send, recv, d):
        return pltpu.make_async_remote_copy(
            src_ref=src,
            dst_ref=dst,
            send_sem=send,
            recv_sem=recv,
            device_id=(ix + d[0], iy + d[1], iz + d[2]),
            device_id_type=MESH,
        )

    def copies(f, d):
        dx, dy, dz = d
        k = code(*d)
        if dz != 0:
            src = z_out.at[f, y_from(dy)]
        else:
            src = (R, C)[f].at[x_from(dx), y_from(dy)]
        send, recv = ((send_r, recv_r), (send_c, recv_c))[f]
        out = [remote(src, landing(f, d), send.at[k], recv.at[k], d)]
        if f == 1:
            out.append(remote(e_out, e_in.at[code(-dx, -dy, -dz)], send_e.at[k], recv_e.at[k], d))
        return out

    def start_all(f):
        for d in DIRS:

            @pl.when(inside(d))
            def _():
                for c in copies(f, d):
                    c.start()

    def wait_all(f):
        for d in DIRS:

            @pl.when(inside(tuple(-a for a in d)))
            def _():
                for c in copies(f, d):
                    c.wait_recv()

    def wait_sent(f):
        for d in DIRS:

            @pl.when(inside(d))
            def _():
                for c in copies(f, d):
                    c.wait_send()

    for d in DIRS:

        @pl.when(jnp.logical_not(inside(tuple(-a for a in d))))
        def _():
            for f in (0, 1):
                ref = landing(f, d)
                ref[...] = jnp.zeros(ref.shape, f32)
            e_in[code(*(-a for a in d))] = jnp.zeros((1, bz), f32)

    lane = lax.broadcasted_iota(jnp.int32, (ey, bz), 1)
    row = lax.broadcasted_iota(jnp.int32, (ey, bz), 0)
    odd_lane, odd_row = lane % 2 == 1, row % 2 == 1
    lane_y = lane[:by]

    def up_y(v, k=1):
        return pltpu.roll(v, k, 0)

    def dn_y(v, k=1):
        return pltpu.roll(v, ey - k, 0)

    def spin(v, k):
        k = k % bz
        return v if k == 0 else pltpu.roll(v, k, 1)

    def up_z(v, k=1):
        return pltpu.roll(v, k, 1)

    def dn_z(v, k=1):
        return pltpu.roll(v, bz - k, 1)

    for load in loads[:3]:
        load.wait()
    own_limit = ext_ref[0].astype(f32)
    e_out[...] = jnp.broadcast_to(own_limit, (1, bz))
    for f, field in ((1, C), (0, R)):
        packed = jnp.zeros((by, bz), f32)
        for k in range(bx):
            moved = spin(field[lo_x + k, :by], 2 * HALO * k + HALO)
            packed = jnp.where(lane_y // (2 * HALO) == k, moved, packed)
        z_out[f] = packed

    def total(v):
        return jnp.sum(v, axis=(0, 1), keepdims=True)

    acc = R[lo_x, :by]
    for k in range(1, bx):
        acc = acc + R[lo_x + k, :by]
    m0 = total(jnp.where(lane_y.astype(f32) < own_limit, acc, 0.0))
    early_row = jnp.broadcast_to(m0, (1, bz))
    early_out[...] = early_row
    early[pl.ds(me, 1)] = early_row[None]

    def remote_row(out, into, base, device):
        return pltpu.make_async_remote_copy(
            src_ref=out,
            dst_ref=into.at[me],
            send_sem=send_g.at[base],
            recv_sem=recv_g.at[base],
            device_id=device,
            device_id_type=MESH,
        )

    def spread(out, into, base):
        everyone(lambda device: remote_row(out, into, base, device).start())

    def collect(into, base):
        part = into.at[pl.ds(0, n - 1)]
        pltpu.make_async_copy(part, part, recv_g.at[base]).wait()
        pltpu.make_async_copy(part, part, send_g.at[base]).wait()

    pl.semaphore_wait(barrier, n - 1)
    start_all(1)
    spread(early_out, early, 0)
    start_all(0)

    loads[3].wait()
    L = factor_ref[...].astype(f32)
    ri = lax.broadcasted_iota(jnp.int32, (n, n), 0)
    ci = lax.broadcasted_iota(jnp.int32, (n, n), 1)
    eye = ri == ci
    X = jnp.where(eye, 1.0 / jnp.where(eye, L, 1.0), 0.0)
    s = 1
    while s < n:
        pick = (ri // (2 * s) == ci // (2 * s)) & (ri % (2 * s) >= s) & (ci % (2 * s) < s)
        low = jnp.where(pick, L, 0.0)
        X = X - jnp.dot(
            X,
            jnp.dot(low, X, precision=HIGH, preferred_element_type=f32),
            precision=HIGH,
            preferred_element_type=f32,
        )
        s *= 2
    inverse = lax.dot_general(
        X, X, (((0,), (0,)), ((), ())), precision=HIGH, preferred_element_type=f32
    )

    one_lane = lax.broadcasted_iota(jnp.int32, (1, bz), 1)
    bands = ((0, by), (1, HALO), (-1, HALO))

    def tables(value):
        rows = {
            (dx, dy, dz): value(dx, dy, dz)
            for dx in (-1, 0, 1)
            for dy in (-1, 0, 1)
            for dz in (-1, 0, 1)
        }
        out = [
            jnp.concatenate(
                [jnp.broadcast_to(rows[dx, dy, 0], (count, bz)) for dy, count in bands], axis=0
            )
            for dx in (-1, 0, 1)
        ]
        for pattern in edge.patterns:
            parts = []
            for dy, count in bands:
                line = None
                for j, key in enumerate(pattern):
                    if key is None:
                        continue
                    dx, start = key[0] - 1, GROUP * j
                    if key[1] == 0:
                        here = jnp.where(
                            one_lane < start + HALO, rows[dx, dy, -1], rows[dx, dy, 0]
                        )
                    else:
                        here = jnp.where(
                            one_lane < start + 2 * HALO, rows[dx, dy, 0], rows[dx, dy, 1]
                        )
                    line = here if line is None else jnp.where(one_lane >= start, here, line)
                parts.append(jnp.broadcast_to(line, (count, bz)))
            out.append(jnp.concatenate(parts, axis=0))
        return out

    def depths():
        plain = one_lane
        out = [plain] * 3
        for pattern in edge.patterns:
            line = None
            for j, key in enumerate(pattern):
                off = one_lane - GROUP * j
                if key is None:
                    here = jnp.full((1, bz), bz, jnp.int32)
                elif key[1] == 0:
                    here = jnp.where(off < HALO, off + bz - HALO, off - HALO)
                else:
                    here = jnp.where(off < 2 * HALO, off + bz - 2 * HALO, off - 2 * HALO)
                line = here if line is None else jnp.where(off >= 0, here, line)
            line = jnp.where(one_lane >= GROUP * edge.places, bz, line)
            out.append(line)
        return out

    def flag_of(i):
        return edge.block(i)[0] if i < ex else 3 + edge.pattern_of[i - ex]

    def build_edges(f, field):
        for t in range(tiles):
            acc = None
            for j in range(edge.places):
                slab = edge.slab(t, j)
                start = GROUP * j
                if slab is None:
                    acc = jnp.where(lane >= start, 0.0, acc)
                    break
                s, side = slab
                which, k = edge.block(s)
                at = 2 * HALO * k
                if side == 0:
                    own = spin(field[s], start + HALO)
                    far = spin(z_in[f, 1, which], start - at)
                    here = jnp.where(lane < start + HALO, far, own)
                else:
                    own = spin(field[s], start + 2 * HALO - bz)
                    far = spin(z_in[f, 0, which], start + HALO - at)
                    here = jnp.where(lane < start + 2 * HALO, own, far)
                acc = here if acc is None else jnp.where(lane >= start, here, acc)
            field[ex + t] = jnp.where(lane < GROUP * edge.places, acc, 0.0)

    def pool_yz(v):
        v = v + jnp.where(odd_row, up_y(v), dn_y(v))
        return v + jnp.where(odd_lane, up_z(v), dn_z(v))

    def walk(load, ref, lo, hi, emit):
        def one(i, v, gx, gx_next):
            gy = FY[i] * (v - up_y(v))
            gz = FZ[i] * (v - up_z(v))
            emit(i, v, (gx - gx_next) + ((gy - dn_y(gy)) + (gz - dn_z(gz))))

        before, v = load(lo - 1), load(lo)
        gx = ref[lo] * (v - before)
        for i in range(lo, hi):
            after = load(i + 1)
            gx_next = ref[i + 1] * (after - v)
            one(i, v, gx, gx_next)
            v, gx = after, gx_next
        before, v = spin(load(ex + tiles - 1), GROUP), load(ex)
        first = gx = ref[ex] * (v - before)
        for t in range(tiles):
            i = ex + t
            if t < tiles - 1:
                after = load(i + 1)
                gx_next = ref[i + 1] * (after - v)
            else:
                after, gx_next = None, spin(first, -GROUP)
            one(i, v, gx, gx_next)
            v, gx = after, gx_next

    wait_all(1)

    def limit(dx, dy, dz):
        return e_out[...] if (dx, dy, dz) == (0, 0, 0) else e_in[code(dx, dy, dz)]

    for k, (a, z) in enumerate(zip(tables(limit), depths())):
        z_f, even_f = z.astype(f32), (z - z % 2).astype(f32)
        FL[k] = (z_f < a).astype(f32)
        F1[k] = (even_f < a).astype(f32)

    build_edges(1, C)
    every = list(range(ex)) + list(range(ex, ex + tiles))
    for i in every:
        c = C[i]
        if i != 0:
            before = spin(C[ex + tiles - 1], GROUP) if i == ex else C[i - 1]
            FX[i] = 0.5 * (before + c)
        FY[i] = 0.5 * (c + up_y(c))
        FZ[i] = 0.5 * (c + up_z(c))
    for i in list(range(1, ex - 1)) + list(range(ex, ex + tiles)):
        fy, fz = FY[i], FZ[i]
        after = spin(FX[ex], -GROUP) if i == ex + tiles - 1 else FX[i + 1]
        diagonal = (FX[i] + after) + (fy + dn_y(fy)) + (fz + dn_z(fz))
        fl = FL[flag_of(i)]
        INV[i] = OMEGA * fl / (diagonal + 1.0 - fl)
    pairs, edge_pairs = ex // 2, tiles // 2
    for q in range(pairs + edge_pairs):
        C1[q] = pool_yz(C[2 * q] + C[2 * q + 1]) * 0.125
    for q in list(range(1, pairs - 1)) + list(range(pairs, pairs + edge_pairs)):
        c = C1[q]
        before = spin(C1[pairs + edge_pairs - 1], GROUP) if q == pairs else C1[q - 1]
        after = spin(C1[pairs], -GROUP) if q == pairs + edge_pairs - 1 else C1[q + 1]
        diagonal = 3.0 * c + 0.5 * (
            (before + after) + (up_y(c, 2) + dn_y(c, 2)) + (up_z(c, 2) + dn_z(c, 2))
        )
        fl = F1[flag_of(2 * q)]
        IC[q] = OMEGA * fl / (4.0 * diagonal + 1.0 - fl)

    off = lane_y % GROUP
    slot0 = (lane_y // GROUP) * tiles

    def core_edge(t, lo_off, hi_off):
        slot = slot0 + t
        low = (slot >= lo_x) & (slot < hi_x) & lo_off
        high = (slot >= ex + lo_x) & (slot < ex + hi_x) & hi_off
        return (low | high) & (lane_y < GROUP * edge.places)

    core_off = (off >= HALO) & (off < 2 * HALO)
    core_tiles = [core_edge(t, core_off, core_off) for t in range(tiles)]
    core_lanes = (lane_y >= HALO) & (lane_y < bz - HALO)

    flux_z = FZ[lo_x, :by]
    flux_y = FY[lo_x]
    for i in range(lo_x + 1, hi_x):
        flux_z = flux_z + FZ[i, :by]
        flux_y = flux_y + FY[i]
    fl = FL[1]
    fl_up, fl_core = up_y(fl), fl[:by]
    step = fl_core - up_z(fl)[:by]
    inner = jnp.where(lane_y >= 1, flux_z * (step * step), 0.0)
    none = jnp.logical_and(off < 0, off >= 0)
    low_face = [core_edge(t, off == HALO, none) for t in range(tiles)]
    high_face = [core_edge(t, none, off == 2 * HALO) for t in range(tiles)]
    sides = {}

    def put(d, alone, shared):
        sides[d] = (total(alone), total(shared))

    alone = FX[lo_x, :by] * fl_core
    put((-1, 0, 0), alone, alone * FL[0, :by])
    alone = FX[hi_x, :by] * fl_core
    put((1, 0, 0), alone, alone * FL[2, :by])
    alone = jnp.where(row == 0, flux_y * fl, 0.0)
    put((0, -1, 0), alone, alone * fl_up)
    alone = jnp.where(row == by, flux_y * fl_up, 0.0)
    put((0, 1, 0), alone, alone * fl)
    zeros = jnp.zeros((by, bz), f32)
    parts = [zeros] * 4
    for t in range(tiles):
        f_edge = FL[3 + edge.pattern_of[t]]
        f_here, f_up = f_edge[:by], up_z(f_edge)[:by]
        fz = FZ[ex + t, :by]
        a = jnp.where(low_face[t], fz * f_here, 0.0)
        b = jnp.where(high_face[t], fz * f_up, 0.0)
        parts = [parts[0] + a, parts[1] + a * f_up, parts[2] + b, parts[3] + b * f_here]
    put((0, 0, -1), parts[0], parts[1])
    put((0, 0, 1), parts[2], parts[3])

    scalars = 8
    width = late.shape[-1]
    base = scalars if width == bz else bz
    col = lax.broadcasted_iota(jnp.int32, (1, width), 1)
    diagonal = total(inner)
    late_row = jnp.zeros((1, width), f32)
    for (dx, dy, dz), (alone, shared) in sides.items():
        diagonal = diagonal + alone
        other = ((ix + dx) * ngy + iy + dy) * ngz + iz + dz
        valid = inside((dx, dy, dz))
        late_row = late_row - jnp.where((col == base + other) & valid, shared, 0.0)
    late_row = late_row + jnp.where(col == base + me, diagonal, 0.0)

    wait_all(0)
    build_edges(0, R)

    def sized(lo, hi):
        return list(range(lo, hi)) + list(range(ex, ex + tiles))

    def cycle(field, lo, hi, finish):
        even = (lo - 1) // 2 * 2
        stop = (hi + 2) // 2 * 2
        held = {}

        def first(i):
            return INV[i] * field[i]

        def coarse(i, v, lv):
            gap = FL[flag_of(i)] * (field[i] - lv)
            if i % 2 == 0:
                held[0] = (v, gap)
                return
            below = IC[i // 2] * pool_yz(held[0][1] + gap)
            for at, w in ((i - 1, held[0][0]), (i, v)):
                SEC[at] = w + FL[flag_of(at)] * below

        walk(first, FX, even, stop, coarse)
        walk(
            lambda i: SEC[i],
            FX,
            lo,
            hi,
            lambda i, v, lv: finish(i, v + INV[i] * (field[i] - lv)),
        )

    def solve(means):
        y_row = jnp.sum(inverse * means, axis=0, keepdims=True)
        y_col = jnp.sum(jnp.where(eye, y_row, 0.0), axis=1, keepdims=True)
        return y_row, y_col

    def block_row(dx, dy, dz):
        def near(at, step, count):
            return jnp.clip(at + step, 0, count - 1)

        b = (near(ix, dx, ngx) * ngy + near(iy, dy, ngy)) * ngz + near(iz, dz, ngz)
        return YB[pl.ds(b, 1)]

    def spread_blocks(y_col):
        YB[...] = jnp.broadcast_to(y_col, (n, bz))
        for k, v in enumerate(tables(block_row)):
            EY[k] = FL[k] * v

    cells = bx * by * bz
    collect(early, 0)
    m0_col = early[:, 0, 0:1]
    _, y_col = solve(m0_col * (1.0 / cells))
    spread_blocks(y_col)

    def keep_direction(i, v):
        D0[i] = v + EY[flag_of(i)]

    cycle(R, 4, ex - 4, keep_direction)

    sums = [[zeros, zeros] for _ in range(7)]

    def add(i, k, v):
        if i < ex:
            if lo_x <= i < hi_x:
                sums[k][0] = sums[k][0] + v()
        else:
            sums[k][1] = sums[k][1] + jnp.where(core_tiles[i - ex], v(), 0.0)

    def keep_image(i, v, lv):
        w = FL[flag_of(i)] * lv
        W[i] = w
        add(i, 0, lambda: R[i, :by] * v[:by])
        add(i, 1, lambda: w[:by] * v[:by])
        add(i, 2, lambda: w[:by])

    walk(lambda i: D0[i], FX, 5, ex - 5, keep_image)

    def keep_second(i, v):
        U[i] = v
        add(i, 3, lambda: W[i, :by] * v[:by])
        add(i, 4, lambda: R[i, :by] * v[:by])

    cycle(W, 7, ex - 7, keep_second)

    def keep_third(i, v, lv):
        q = FL[flag_of(i)] * lv
        Q[i] = q
        add(i, 5, lambda: q[:by] * v[:by])
        add(i, 6, lambda: q[:by])

    walk(lambda i: U[i], FX, lo_x, hi_x, keep_third)

    for k, (a, b) in enumerate(sums):
        part = total(jnp.where(core_lanes, a, 0.0) + b)
        late_row = jnp.where(col == k, part, late_row)
    late_out[...] = late_row
    late[pl.ds(me, 1)] = late_row[None]
    spread(late_out, late, 1)
    collect(late, 1)

    rows = late[:, 0, :]
    y_row, y_col = solve(rows[:, 2:3] * (1.0 / cells))
    spread_blocks(y_col)
    plain = jnp.sum(rows, axis=0, keepdims=True)
    weighted = jnp.sum(rows * y_col, axis=0, keepdims=True)

    def pick(line, k):
        return jnp.sum(line[:, k : k + 1], axis=(0, 1), keepdims=True)

    rz, dad = pick(plain, 0), pick(plain, 1)
    y_m0 = total(m0_col * y_col)
    w_u = pick(plain, 3) + pick(weighted, 2)
    r_u = pick(plain, 4) + y_m0
    u_q = (
        pick(plain, 5)
        + 2.0 * pick(weighted, 6)
        + total(weighted[:, base : base + n] * y_row)
    )
    alpha = rz / dad
    new = (rz - alpha * dad) + alpha * (alpha * w_u - r_u)
    beta = new / rz
    grow = 1.0 + beta
    dad1 = grow * grow * dad - 2.0 * alpha * grow * w_u + alpha * alpha * u_q
    alpha1 = new / dad1
    c1 = alpha + alpha1 * grow
    c2 = alpha * alpha1

    edges = {}

    def results(i, v, lv):
        fl = FL[flag_of(i)][:by]
        sol = c1 * D0[i, :by] - c2 * (U[i, :by] + v[:by])
        res = fl * R[i, :by] - c1 * W[i, :by] + c2 * (Q[i, :by] + fl * lv[:by])
        if i < ex:
            sol_ref[i - lo_x], res_ref[i - lo_x] = sol, res
        else:
            SEC[i, :by], D0[i, :by] = sol, res

    walk(lambda i: EY[flag_of(i)], FX, lo_x, hi_x, results)
    for x in range(bx):
        tl, jl = edge.place(lo_x + x, 0)
        th, jh = edge.place(lo_x + x, 1)
        for ref, held in ((sol_ref, SEC), (res_ref, D0)):
            low = spin(held[ex + tl, :by], -(GROUP * jl + HALO))
            high = spin(held[ex + th, :by], bz - HALO - (GROUP * jh + HALO))
            ref[x] = jnp.where(
                lane_y < HALO, low, jnp.where(lane_y >= bz - HALO, high, ref[x])
            )
    wait_sent(1)
    wait_sent(0)


def solution(mesh):
    counts = (mesh.shape["gx"], mesh.shape["gy"], mesh.shape["gz"])
    n = counts[0] * counts[1] * counts[2]

    def on_device(right_side, conductance, extents, coarse_factor):
        f32 = jnp.float32
        bx, by, bz = right_side.shape
        ex, ey = bx + 2 * HALO, by + 2 * HALO
        edge = Edge(bx, bz)
        slabs = ex + edge.tiles
        width = bz if n + 8 <= bz else bz + -(-n // 128) * 128
        vm = lambda *shape: pltpu.VMEM(shape, f32)
        field = vm(slabs, ey, bz)
        half = vm(slabs // 2, ey, bz)
        flags = vm(3 + len(edge.patterns), ey, bz)
        dma = pltpu.SemaphoreType.DMA
        scratch = [
            field,
            field,
            pltpu.VMEM(extents.shape, extents.dtype),
            pltpu.VMEM(coarse_factor.shape, coarse_factor.dtype),
            vm(1, bz),
            vm(27, 1, bz),
            vm(2, by, bz),
            vm(2, 2, 3, ey, bz),
            vm(1, bz),
            vm(n, 1, bz),
            vm(1, width),
            vm(n, 1, width),
            flags,
            flags,
            field,
            field,
            field,
            field,
            half,
            half,
            field,
            field,
            field,
            field,
            field,
            vm(n, bz),
            flags,
            dma((27,)),
            dma((27,)),
            dma((27,)),
            dma((27,)),
            dma((27,)),
            dma((27,)),
            dma((2,)),
            dma((2,)),
            dma((4,)),
        ]
        block = vm(bx, by, bz)
        whole = pl.BlockSpec(memory_space=pltpu.VMEM)
        outer = pl.BlockSpec(memory_space=pltpu.HBM)
        return pl.pallas_call(
            functools.partial(kernel, counts),
            out_shape=(block, block),
            in_specs=[outer, outer, outer, outer],
            out_specs=(whole, whole),
            scratch_shapes=scratch,
            compiler_params=pltpu.CompilerParams(
                collective_id=0, has_side_effects=True, vmem_limit_bytes=60000000
            ),
        )(right_side, conductance, extents, coarse_factor)

    in_specs = (P("gx", "gy", "gz"), P("gx", "gy", "gz"), P("gx", "gy", "gz"), P())
    out_specs = (P("gx", "gy", "gz"), P("gx", "gy", "gz"))
    return jax.shard_map(
        on_device, mesh=mesh, in_specs=in_specs, out_specs=out_specs, check_vma=False
    )
```

time: 27.6 us -> 29.4 us (1.065)
  Pallas kernels: 24.9 us -> 26.7 us
    pallas_call x1, Pallas kernels: 24.9 us -> 26.7 us  [on_device(): pl.pallas_call(functools.partial(kernel, counts), out_shape=(block, block...]
where the time goes in v1:
time: 29.4 us; the launch traced here: 29.3 us
  Pallas kernels  26.7 us (91%)
  between operations  1.28 us (4%)
  local copies, waits for them, and re-layouts  1.26 us (4%)
    pallas_call x1, Pallas kernels, on_device(): pl.pallas_call(functools.partial(kernel, counts), out_shape=(block, block...  26.7 us
    unnamed x2, local copies, waits for them, and re-layouts  1.26 us

profile of v1, /device:TPU:0, one launch (start us, length us, event | category | flops | bytes accessed | tf_op | source)
XLA Modules:
  0.0 29.3 jit_solution(1574709311587171901)
XLA Ops:
  1.3 26.7 %shard_map.59 = (f32[8,16,128]{2,1,0:T(8,128)S(1)}, f32[8,16,128]{2,1,0:T(8,128)S(1)}) custom-call(f32[8,16,128]{2,1,0:T(8,128)} %rhs_hbm.1, f32[8,16,128]{2,1,0:T(8,128)} %cond_hbm.1, s32[1,1,1]{2,1,0:T(1,128)S(6)} %copy.10.ext_hbm, bf16[32,32]{1,0:T(8,128)(2,1)} %factor_hbm.1), custom_call_target="tpu_custom_call" | custom-call | tf_op jit(solution)/shard_map/pallas_call | solution.py:758
  28.0 0.6 %copy.8 = f32[8,16,128]{2,1,0:T(8,128)} copy(f32[8,16,128]{2,1,0:T(8,128)S(1)} %get-tuple-element.2) | data formatting | bytes 131072
  28.6 0.6 %copy.9 = f32[8,16,128]{2,1,0:T(8,128)} copy(f32[8,16,128]{2,1,0:T(8,128)S(1)} %get-tuple-element.3) | data formatting | bytes 131072

commit v2 on v1

--- a/solution.py
+++ b/solution.py
@@ -10,6 +10,7 @@
 OMEGA = 0.8
 HALO = 8
 GROUP = 3 * HALO
+SPAN = 16
 MESH = pl.DeviceIdType.MESH
 HIGH = lax.Precision.HIGHEST
 DIRS = [
@@ -419,30 +420,75 @@
         v = v + jnp.where(odd_row, up_y(v), dn_y(v))
         return v + jnp.where(odd_lane, up_z(v), dn_z(v))
 
-    def walk(load, ref, lo, hi, emit):
-        def one(i, v, gx, gx_next):
-            gy = FY[i] * (v - up_y(v))
-            gz = FZ[i] * (v - up_z(v))
-            emit(i, v, (gx - gx_next) + ((gy - dn_y(gy)) + (gz - dn_z(gz))))
-
-        before, v = load(lo - 1), load(lo)
-        gx = ref[lo] * (v - before)
-        for i in range(lo, hi):
-            after = load(i + 1)
-            gx_next = ref[i + 1] * (after - v)
-            one(i, v, gx, gx_next)
-            v, gx = after, gx_next
-        before, v = spin(load(ex + tiles - 1), GROUP), load(ex)
-        first = gx = ref[ex] * (v - before)
-        for t in range(tiles):
-            i = ex + t
-            if t < tiles - 1:
-                after = load(i + 1)
-                gx_next = ref[i + 1] * (after - v)
+    def groups(lo, hi):
+        out = []
+        for a, b in ((lo, hi), (ex, ex + tiles)):
+            at = a
+            while at < b:
+                stop = min(b, at + SPAN - (at - a) % SPAN)
+                out.append(list(range(at, stop)))
+                at = stop
+        return out
+
+    def around(i):
+        last = ex + tiles - 1
+        before = (last, GROUP) if i == ex else (i - 1, 0)
+        after = (ex, -GROUP) if i == last else (i + 1, 0)
+        return before, after
+
+    def faces(load, group):
+        v, turned_v = {}, {}
+        for i in group:
+            v[i] = load(i)
+        for at, k in (around(group[0])[0], around(group[-1])[1]):
+            turned_v[at, k] = v[at] if k == 0 and at in v else spin(load(at), k)
+        up = {i: up_z(v[i]) for i in group}
+        yield
+        gz, dn = {}, {}
+        for i in group:
+            gz[i] = FZ[i] * (v[i] - up[i])
+            dn[i] = dn_z(gz[i])
+        yield
+        out = {}
+        (b, kb), _ = around(group[0])
+        gx = FX[group[0]] * (v[group[0]] - turned_v[b, kb])
+        for i in group:
+            if i == group[-1]:
+                a, ka = around(i)[1]
+                after = turned_v[a, ka]
             else:
-                after, gx_next = None, spin(first, -GROUP)
-            one(i, v, gx, gx_next)
-            v, gx = after, gx_next
+                after = v[i + 1]
+            gx_next = FX[i + 1] * (after - v[i])
+            gy = FY[i] * (v[i] - up_y(v[i]))
+            out[i] = (v[i], (gx - gx_next) + ((gy - dn_y(gy)) + (gz[i] - dn[i])))
+            gx = gx_next
+        return out
+
+    def reads(name, group):
+        return {(name, i) for i in group} | {
+            (name, around(group[0])[0][0]),
+            (name, around(group[-1])[1][0]),
+        }
+
+    def run(items):
+        done, open_items, at = set(), [], 0
+        while at < len(items) or open_items:
+            still = []
+            for gen, gives in open_items:
+                try:
+                    next(gen)
+                    still.append((gen, gives))
+                except StopIteration:
+                    done |= gives
+            open_items = still
+            if at < len(items) and items[at][1] <= done:
+                gen, _, gives = items[at]
+                at += 1
+                try:
+                    next(gen)
+                    open_items.append((gen, gives))
+                except StopIteration:
+                    done |= gives
 
     wait_all(1)
 
@@ -463,10 +509,10 @@
             FX[i] = 0.5 * (before + c)
         FY[i] = 0.5 * (c + up_y(c))
         FZ[i] = 0.5 * (c + up_z(c))
+    FX[ex + tiles] = spin(FX[ex], -GROUP)
     for i in list(range(1, ex - 1)) + list(range(ex, ex + tiles)):
         fy, fz = FY[i], FZ[i]
-        after = spin(FX[ex], -GROUP) if i == ex + tiles - 1 else FX[i + 1]
-        diagonal = (FX[i] + after) + (fy + dn_y(fy)) + (fz + dn_z(fz))
+        diagonal = (FX[i] + FX[i + 1]) + (fy + dn_y(fy)) + (fz + dn_z(fz))
         fl = FL[flag_of(i)]
         INV[i] = OMEGA * fl / (diagonal + 1.0 - fl)
     pairs, edge_pairs = ex // 2, tiles // 2
@@ -548,35 +594,6 @@
     wait_all(0)
     build_edges(0, R)
 
-    def sized(lo, hi):
-        return list(range(lo, hi)) + list(range(ex, ex + tiles))
-
-    def cycle(field, lo, hi, finish):
-        even = (lo - 1) // 2 * 2
-        stop = (hi + 2) // 2 * 2
-        held = {}
-
-        def first(i):
-            return INV[i] * field[i]
-
-        def coarse(i, v, lv):
-            gap = FL[flag_of(i)] * (field[i] - lv)
-            if i % 2 == 0:
-                held[0] = (v, gap)
-                return
-            below = IC[i // 2] * pool_yz(held[0][1] + gap)
-            for at, w in ((i - 1, held[0][0]), (i, v)):
-                SEC[at] = w + FL[flag_of(at)] * below
-
-        walk(first, FX, even, stop, coarse)
-        walk(
-            lambda i: SEC[i],
-            FX,
-            lo,
-            hi,
-            lambda i, v, lv: finish(i, v + INV[i] * (field[i] - lv)),
-        )
-
     def solve(means):
         y_row = jnp.sum(inverse * means, axis=0, keepdims=True)
         y_col = jnp.sum(jnp.where(eye, y_row, 0.0), axis=1, keepdims=True)
@@ -597,50 +614,108 @@
     cells = bx * by * bz
     collect(early, 0)
     m0_col = early[:, 0, 0:1]
-    _, y_col = solve(m0_col * (1.0 / cells))
-    spread_blocks(y_col)
-
-    def keep_direction(i, v):
-        D0[i] = v + EY[flag_of(i)]
-
-    cycle(R, 4, ex - 4, keep_direction)
-
+
+    def first_solve():
+        y_row = jnp.sum(inverse * (m0_col * (1.0 / cells)), axis=0, keepdims=True)
+        yield
+        y_col = jnp.sum(jnp.where(eye, y_row, 0.0), axis=1, keepdims=True)
+        yield
+        yield
+        spread_blocks(y_col)
+
+    items = [(first_solve(), set(), {"blocks"})]
     sums = [[zeros, zeros] for _ in range(7)]
+    parts = {}
 
     def add(i, k, v):
         if i < ex:
             if lo_x <= i < hi_x:
-                sums[k][0] = sums[k][0] + v()
+                sums[k][0] = sums[k][0] + v
         else:
-            sums[k][1] = sums[k][1] + jnp.where(core_tiles[i - ex], v(), 0.0)
+            sums[k][1] = sums[k][1] + jnp.where(core_tiles[i - ex], v, 0.0)
+
+    def coarse(field, group):
+        found = yield from faces(lambda i: INV[i] * field[i], group)
+        pooled = {}
+        for i in group[::2]:
+            gap = FL[flag_of(i)] * (field[i] - found[i][1])
+            gap = gap + FL[flag_of(i + 1)] * (field[i + 1] - found[i + 1][1])
+            gap = gap + jnp.where(odd_row, up_y(gap), dn_y(gap))
+            pooled[i] = (gap, up_z(gap), dn_z(gap))
+        yield
+        for i in group[::2]:
+            gap, up, dn = pooled[i]
+            below = IC[i // 2] * (gap + jnp.where(odd_lane, up, dn))
+            for at in (i, i + 1):
+                SEC[at] = found[at][0] + FL[flag_of(at)] * below
+
+    def smooth(field, group, keep):
+        found = yield from faces(lambda i: SEC[i], group)
+        for i in group:
+            v, lv = found[i]
+            keep(i, v + INV[i] * (field[i] - lv))
+
+    def image(load, group, keep):
+        found = yield from faces(load, group)
+        for i in group:
+            keep(i, *found[i])
+
+    def add_cycle(field, source, name, lo, hi, keep, extra):
+        even, stop = (lo - 1) // 2 * 2, (hi + 2) // 2 * 2
+        for group in groups(even, stop):
+            needs = set() if source is None else reads(source, group)
+            items.append((coarse(field, group), needs, {(name + "s", i) for i in group}))
+        for group in groups(lo, hi):
+            needs = reads(name + "s", group) | extra
+            items.append((smooth(field, group, keep), needs, {(name, i) for i in group}))
+
+    def keep_direction(i, v):
+        D0[i] = v + EY[flag_of(i)]
 
     def keep_image(i, v, lv):
         w = FL[flag_of(i)] * lv
         W[i] = w
-        add(i, 0, lambda: R[i, :by] * v[:by])
-        add(i, 1, lambda: w[:by] * v[:by])
-        add(i, 2, lambda: w[:by])
-
-    walk(lambda i: D0[i], FX, 5, ex - 5, keep_image)
+        add(i, 0, R[i, :by] * v[:by])
+        add(i, 1, w[:by] * v[:by])
+        add(i, 2, w[:by])
 
     def keep_second(i, v):
         U[i] = v
-        add(i, 3, lambda: W[i, :by] * v[:by])
-        add(i, 4, lambda: R[i, :by] * v[:by])
-
-    cycle(W, 7, ex - 7, keep_second)
+        add(i, 3, W[i, :by] * v[:by])
+        add(i, 4, R[i, :by] * v[:by])
 
     def keep_third(i, v, lv):
-        q = FL[flag_of(i)] * lv
-        Q[i] = q
-        add(i, 5, lambda: q[:by] * v[:by])
-        add(i, 6, lambda: q[:by])
-
-    walk(lambda i: U[i], FX, lo_x, hi_x, keep_third)
-
-    for k, (a, b) in enumerate(sums):
-        part = total(jnp.where(core_lanes, a, 0.0) + b)
-        late_row = jnp.where(col == k, part, late_row)
+        q = FL[flag_of(i)][:by] * lv[:by]
+        Q[i, :by] = q
+        add(i, 5, q * v[:by])
+        add(i, 6, q)
+
+    def gather_sums(which):
+        for k in which:
+            a, b = sums[k]
+            parts[k] = total(jnp.where(core_lanes, a, 0.0) + b)
+        yield
+
+    def core_of(name):
+        return {(name, i) for i in range(lo_x, hi_x)} | {(name, ex + t) for t in range(tiles)}
+
+    add_cycle(R, None, "d", 4, ex - 4, keep_direction, {"blocks"})
+    for group in groups(5, ex - 5):
+        items.append(
+            (image(lambda i: D0[i], group, keep_image), reads("d", group), {("w", i) for i in group})
+        )
+    add_cycle(W, "w", "u", 7, ex - 7, keep_second, set())
+    items.append((gather_sums(range(3)), core_of("w"), set()))
+    for group in groups(lo_x, hi_x):
+        items.append(
+            (image(lambda i: U[i], group, keep_third), reads("u", group), {("q", i) for i in group})
+        )
+    items.append((gather_sums(range(3, 5)), core_of("u"), set()))
+    items.append((gather_sums(range(5, 7)), core_of("q"), set()))
+    run(items)
+
+    for k in range(7):
+        late_row = jnp.where(col == k, parts[k], late_row)
     late_out[...] = late_row
     late[pl.ds(me, 1)] = late_row[None]
     spread(late_out, late, 1)
@@ -673,8 +748,6 @@
     c1 = alpha + alpha1 * grow
     c2 = alpha * alpha1
 
-    edges = {}
-
     def results(i, v, lv):
         fl = FL[flag_of(i)][:by]
         sol = c1 * D0[i, :by] - c2 * (U[i, :by] + v[:by])
@@ -682,13 +755,18 @@
         if i < ex:
             sol_ref[i - lo_x], res_ref[i - lo_x] = sol, res
         else:
-            SEC[i, :by], D0[i, :by] = sol, res
-
-    walk(lambda i: EY[flag_of(i)], FX, lo_x, hi_x, results)
+            SEC[i, :by], INV[i, :by] = sol, res
+
+    run(
+        [
+            (image(lambda i: EY[flag_of(i)], group, results), set(), set())
+            for group in groups(lo_x, hi_x)
+        ]
+    )
     for x in range(bx):
         tl, jl = edge.place(lo_x + x, 0)
         th, jh = edge.place(lo_x + x, 1)
-        for ref, held in ((sol_ref, SEC), (res_ref, D0)):
+        for ref, held in ((sol_ref, SEC), (res_ref, INV)):
             low = spin(held[ex + tl, :by], -(GROUP * jl + HALO))
             high = spin(held[ex + th, :by], bz - HALO - (GROUP * jh + HALO))
             ref[x] = jnp.where(
@@ -729,7 +807,7 @@
             vm(n, 1, width),
             flags,
             flags,
-            field,
+            vm(slabs + 1, ey, bz),
             field,
             field,
             field,

time: 29.4 us -> 24.5 us (0.83)
  Pallas kernels: 26.7 us -> 21.7 us
    pallas_call x1, Pallas kernels: 26.7 us -> 21.7 us  [on_device(): pl.pallas_call(functools.partial(kernel, counts), out_shape=(block, block...]
where the time goes in v2:
time: 24.5 us; the launch traced here: 24.3 us
  Pallas kernels  21.7 us (89%)
  between operations  1.28 us (5%)
  local copies, waits for them, and re-layouts  1.26 us (5%)
    pallas_call x1, Pallas kernels, on_device(): pl.pallas_call(functools.partial(kernel, counts), out_shape=(block, block...  21.7 us
    unnamed x2, local copies, waits for them, and re-layouts  1.26 us

profile of v2, /device:TPU:0, one launch (start us, length us, event | category | flops | bytes accessed | tf_op | source)
XLA Modules:
  0.0 24.3 jit_solution(17372365719831305681)
XLA Ops:
  1.3 21.7 %shard_map.59 = (f32[8,16,128]{2,1,0:T(8,128)S(1)}, f32[8,16,128]{2,1,0:T(8,128)S(1)}) custom-call(f32[8,16,128]{2,1,0:T(8,128)} %rhs_hbm.1, f32[8,16,128]{2,1,0:T(8,128)} %cond_hbm.1, s32[1,1,1]{2,1,0:T(1,128)S(6)} %copy.10.ext_hbm, bf16[32,32]{1,0:T(8,128)(2,1)} %factor_hbm.1), custom_call_target="tpu_custom_call" | custom-call | tf_op jit(solution)/shard_map/pallas_call | solution.py:836
  23.0 0.6 %copy.8 = f32[8,16,128]{2,1,0:T(8,128)} copy(f32[8,16,128]{2,1,0:T(8,128)S(1)} %get-tuple-element.2) | data formatting | bytes 131072
  23.7 0.6 %copy.9 = f32[8,16,128]{2,1,0:T(8,128)} copy(f32[8,16,128]{2,1,0:T(8,128)S(1)} %get-tuple-element.3) | data formatting | bytes 131072

commit v3 on v2

--- a/solution.py
+++ b/solution.py
@@ -65,8 +65,7 @@
     cond_hbm,
     ext_hbm,
     factor_hbm,
-    sol_ref,
-    res_ref,
+    both_ref,
     R,
     C,
     ext_ref,
@@ -104,6 +103,7 @@
     recv_g,
     load_sem,
 ):
+    sol_ref, res_ref = both_ref.at[0], both_ref.at[1]
     ngx, ngy, ngz = counts
     n = ngx * ngy * ngz
     ix, iy, iz = lax.axis_index("gx"), lax.axis_index("gy"), lax.axis_index("gz")
@@ -215,29 +215,70 @@
             out.append(remote(e_out, e_in.at[code(-dx, -dy, -dz)], send_e.at[k], recv_e.at[k], d))
         return out
 
-    def start_all(f):
+    odd = ix % 2 == 1
+
+    def corner(d):
+        return d[0] != 0 and d[1] != 0 and d[2] == 0
+
+    def when_sent(f, act):
         for d in DIRS:
 
             @pl.when(inside(d))
             def _():
-                for c in copies(f, d):
-                    c.start()
+                values, *flags = copies(f, d)
+                for c in flags:
+                    act(c)
+                if not corner(d):
+                    act(values)
+                    return
+
+                if d[0] == 1:
+                    act(values)
+                    return
+
+                @pl.when(jnp.logical_not(odd))
+                def _():
+                    act(values)
+
+    def relayed(f, dy):
+        field, k = (R, C)[f], code(-1, dy, 0)
+        send, recv = ((send_r, recv_r), (send_c, recv_c))[f]
+        return remote(
+            field.at[x_from(-1), y_into(dy)],
+            field.at[x_into(-1), y_into(dy)],
+            send.at[k],
+            recv.at[k],
+            (-1, 0, 0),
+        )
+
+    def start_all(f):
+        when_sent(f, lambda c: c.start())
+
+    def relay(f):
+        for dy in (-1, 1):
+
+            @pl.when(inside((0, -dy, 0)) & odd)
+            def _():
+                for c in copies(f, (0, dy, 0)):
+                    c.wait_recv()
+                relayed(f, dy).start()
 
     def wait_all(f):
         for d in DIRS:
-
-            @pl.when(inside(tuple(-a for a in d)))
+            ok = inside(tuple(-a for a in d))
+
+            @pl.when(ok & jnp.logical_not(odd) if d[0] == 0 and d[2] == 0 else ok)
             def _():
                 for c in copies(f, d):
                     c.wait_recv()
 
     def wait_sent(f):
-        for d in DIRS:
-
-            @pl.when(inside(d))
+        when_sent(f, lambda c: c.wait_send())
+        for dy in (-1, 1):
+
+            @pl.when(inside((0, -dy, 0)) & odd)
             def _():
-                for c in copies(f, d):
-                    c.wait_send()
+                relayed(f, dy).wait_send()
 
     for d in DIRS:
 
@@ -490,7 +531,9 @@
                 except StopIteration:
                     done |= gives
 
+    relay(1)
     wait_all(1)
+    relay(0)
 
     def limit(dx, dy, dz):
         return e_out[...] if (dx, dy, dz) == (0, 0, 0) else e_in[code(dx, dy, dz)]
@@ -541,55 +584,62 @@
     core_tiles = [core_edge(t, core_off, core_off) for t in range(tiles)]
     core_lanes = (lane_y >= HALO) & (lane_y < bz - HALO)
 
-    flux_z = FZ[lo_x, :by]
-    flux_y = FY[lo_x]
-    for i in range(lo_x + 1, hi_x):
-        flux_z = flux_z + FZ[i, :by]
-        flux_y = flux_y + FY[i]
-    fl = FL[1]
-    fl_up, fl_core = up_y(fl), fl[:by]
-    step = fl_core - up_z(fl)[:by]
-    inner = jnp.where(lane_y >= 1, flux_z * (step * step), 0.0)
-    none = jnp.logical_and(off < 0, off >= 0)
-    low_face = [core_edge(t, off == HALO, none) for t in range(tiles)]
-    high_face = [core_edge(t, none, off == 2 * HALO) for t in range(tiles)]
-    sides = {}
-
-    def put(d, alone, shared):
-        sides[d] = (total(alone), total(shared))
-
-    alone = FX[lo_x, :by] * fl_core
-    put((-1, 0, 0), alone, alone * FL[0, :by])
-    alone = FX[hi_x, :by] * fl_core
-    put((1, 0, 0), alone, alone * FL[2, :by])
-    alone = jnp.where(row == 0, flux_y * fl, 0.0)
-    put((0, -1, 0), alone, alone * fl_up)
-    alone = jnp.where(row == by, flux_y * fl_up, 0.0)
-    put((0, 1, 0), alone, alone * fl)
     zeros = jnp.zeros((by, bz), f32)
-    parts = [zeros] * 4
-    for t in range(tiles):
-        f_edge = FL[3 + edge.pattern_of[t]]
-        f_here, f_up = f_edge[:by], up_z(f_edge)[:by]
-        fz = FZ[ex + t, :by]
-        a = jnp.where(low_face[t], fz * f_here, 0.0)
-        b = jnp.where(high_face[t], fz * f_up, 0.0)
-        parts = [parts[0] + a, parts[1] + a * f_up, parts[2] + b, parts[3] + b * f_here]
-    put((0, 0, -1), parts[0], parts[1])
-    put((0, 0, 1), parts[2], parts[3])
-
     scalars = 8
     width = late.shape[-1]
     base = scalars if width == bz else bz
     col = lax.broadcasted_iota(jnp.int32, (1, width), 1)
-    diagonal = total(inner)
-    late_row = jnp.zeros((1, width), f32)
-    for (dx, dy, dz), (alone, shared) in sides.items():
-        diagonal = diagonal + alone
-        other = ((ix + dx) * ngy + iy + dy) * ngz + iz + dz
-        valid = inside((dx, dy, dz))
-        late_row = late_row - jnp.where((col == base + other) & valid, shared, 0.0)
-    late_row = late_row + jnp.where(col == base + me, diagonal, 0.0)
+    coupling = {}
+
+    def couple():
+        flux_z = FZ[lo_x, :by]
+        flux_y = FY[lo_x]
+        for i in range(lo_x + 1, hi_x):
+            flux_z = flux_z + FZ[i, :by]
+            flux_y = flux_y + FY[i]
+        fl = FL[1]
+        fl_up, fl_core = up_y(fl), fl[:by]
+        step = fl_core - up_z(fl)[:by]
+        inner = jnp.where(lane_y >= 1, flux_z * (step * step), 0.0)
+        none = jnp.logical_and(off < 0, off >= 0)
+        low_face = [core_edge(t, off == HALO, none) for t in range(tiles)]
+        high_face = [core_edge(t, none, off == 2 * HALO) for t in range(tiles)]
+        sides = {}
+
+        def put(d, alone, shared):
+            sides[d] = (total(alone), total(shared))
+
+        alone = FX[lo_x, :by] * fl_core
+        put((-1, 0, 0), alone, alone * FL[0, :by])
+        alone = FX[hi_x, :by] * fl_core
+        put((1, 0, 0), alone, alone * FL[2, :by])
+        alone = jnp.where(row == 0, flux_y * fl, 0.0)
+        put((0, -1, 0), alone, alone * fl_up)
+        alone = jnp.where(row == by, flux_y * fl_up, 0.0)
+        put((0, 1, 0), alone, alone * fl)
+        parts = [zeros] * 4
+        for t in range(tiles):
+            f_edge = FL[3 + edge.pattern_of[t]]
+            f_here, f_up = f_edge[:by], up_z(f_edge)[:by]
+            fz = FZ[ex + t, :by]
+            a = jnp.where(low_face[t], fz * f_here, 0.0)
+            b = jnp.where(high_face[t], fz * f_up, 0.0)
+            parts = [parts[0] + a, parts[1] + a * f_up, parts[2] + b, parts[3] + b * f_here]
+        put((0, 0, -1), parts[0], parts[1])
+        put((0, 0, 1), parts[2], parts[3])
+
+        inner_sum = total(inner)
+        yield
+        yield
+        diagonal = inner_sum
+        late_row = jnp.zeros((1, width), f32)
+        for (dx, dy, dz), (alone, shared) in sides.items():
+            diagonal = diagonal + alone
+            other = ((ix + dx) * ngy + iy + dy) * ngz + iz + dz
+            valid = inside((dx, dy, dz))
+            late_row = late_row - jnp.where((col == base + other) & valid, shared, 0.0)
+        late_row = late_row + jnp.where(col == base + me, diagonal, 0.0)
+        coupling[0] = late_row
 
     wait_all(0)
     build_edges(0, R)
@@ -705,6 +755,7 @@
             (image(lambda i: D0[i], group, keep_image), reads("d", group), {("w", i) for i in group})
         )
     add_cycle(W, "w", "u", 7, ex - 7, keep_second, set())
+    items.append((couple(), set(), set()))
     items.append((gather_sums(range(3)), core_of("w"), set()))
     for group in groups(lo_x, hi_x):
         items.append(
@@ -714,11 +765,14 @@
     items.append((gather_sums(range(5, 7)), core_of("q"), set()))
     run(items)
 
+    late_row = coupling[0]
     for k in range(7):
         late_row = jnp.where(col == k, parts[k], late_row)
     late_out[...] = late_row
     late[pl.ds(me, 1)] = late_row[None]
     spread(late_out, late, 1)
+    wait_sent(1)
+    wait_sent(0)
     collect(late, 1)
 
     rows = late[:, 0, :]
@@ -772,8 +826,6 @@
             ref[x] = jnp.where(
                 lane_y < HALO, low, jnp.where(lane_y >= bz - HALO, high, ref[x])
             )
-    wait_sent(1)
-    wait_sent(0)
 
 
 def solution(mesh):
@@ -830,19 +882,19 @@
             dma((2,)),
             dma((4,)),
         ]
-        block = vm(bx, by, bz)
         whole = pl.BlockSpec(memory_space=pltpu.VMEM)
         outer = pl.BlockSpec(memory_space=pltpu.HBM)
-        return pl.pallas_call(
+        both = pl.pallas_call(
             functools.partial(kernel, counts),
-            out_shape=(block, block),
+            out_shape=vm(2, bx, by, bz),
             in_specs=[outer, outer, outer, outer],
-            out_specs=(whole, whole),
+            out_specs=whole,
             scratch_shapes=scratch,
             compiler_params=pltpu.CompilerParams(
                 collective_id=0, has_side_effects=True, vmem_limit_bytes=60000000
             ),
         )(right_side, conductance, extents, coarse_factor)
+        return both[0], both[1]
 
     in_specs = (P("gx", "gy", "gz"), P("gx", "gy", "gz"), P("gx", "gy", "gz"), P())
     out_specs = (P("gx", "gy", "gz"), P("gx", "gy", "gz"))

time: 24.5 us -> 23.4 us (0.955)
  local copies, waits for them, and re-layouts: 1.26 us -> 0.66 us
  Pallas kernels: 21.7 us -> 21.2 us
    unnamed x2 -> x0, local copies, waits for them, and re-layouts: 1.26 us -> none
    squeeze x0 -> x1, local copies, waits for them, and re-layouts: none -> 0.66 us  [on_device(): return (both[0], both[1])]
    pallas_call x1, Pallas kernels: 21.7 us -> 21.2 us  [on_device(): pl.pallas_call(functools.partial(kernel, counts), out_shape=vm(2, bx, by,...]
where the time goes in v3:
time: 23.4 us; the launch traced here: 23.2 us
  Pallas kernels  21.2 us (91%)
  between operations  1.28 us (5%)
  local copies, waits for them, and re-layouts  0.66 us (3%)
    pallas_call x1, Pallas kernels, on_device(): pl.pallas_call(functools.partial(kernel, counts), out_shape=vm(2, bx, by,...  21.2 us
    squeeze x1, local copies, waits for them, and re-layouts, on_device(): return (both[0], both[1])  0.66 us

profile of v3, /device:TPU:0, one launch (start us, length us, event | category | flops | bytes accessed | tf_op | source)
XLA Modules:
  0.0 23.2 jit_solution(5892583067699239199)
XLA Ops:
  1.3 21.2 %shard_map.59 = f32[2,8,16,128]{3,2,1,0:T(8,128)S(1)} custom-call(f32[8,16,128]{2,1,0:T(8,128)} %rhs_hbm.1, f32[8,16,128]{2,1,0:T(8,128)} %cond_hbm.1, s32[1,1,1]{2,1,0:T(1,128)S(6)} %copy.6.ext_hbm, bf16[32,32]{1,0:T(8,128)(2,1)} %factor_hbm.1), custom_call_target="tpu_custom_call" | custom-call | tf_op jit(solution)/shard_map/pallas_call | solution.py:887
  22.5 0.7 %slice_bitcast_fusion = (f32[8,16,128]{2,1,0:T(8,128)}, f32[8,16,128]{2,1,0:T(8,128)}) fusion(f32[2,8,16,128]{3,2,1,0:T(8,128)S(1)} %shard_map.59), kind=kLoop, calls=%fused_computation | loop fusion | bytes 262144 | tf_op jit(solution)/shard_map/squeeze | solution.py:897

commit v4 on v3

--- a/solution.py
+++ b/solution.py
@@ -10,7 +10,9 @@
 OMEGA = 0.8
 HALO = 8
 GROUP = 3 * HALO
-SPAN = 16
+SPAN = 24
+WIDE = 12
+EDGES = 2
 MESH = pl.DeviceIdType.MESH
 HIGH = lax.Precision.HIGHEST
 DIRS = [
@@ -291,7 +293,8 @@
 
     lane = lax.broadcasted_iota(jnp.int32, (ey, bz), 1)
     row = lax.broadcasted_iota(jnp.int32, (ey, bz), 0)
-    odd_lane, odd_row = lane % 2 == 1, row % 2 == 1
+    odd_lane = lane % 2 == 1
+    odd_row = (row % 2 == 1).reshape(ey // 8, 8, bz)
     lane_y = lane[:by]
 
     def up_y(v, k=1):
@@ -348,6 +351,9 @@
     def collect(into, base):
         part = into.at[pl.ds(0, n - 1)]
         pltpu.make_async_copy(part, part, recv_g.at[base]).wait()
+
+    def spread_done(into, base):
+        part = into.at[pl.ds(0, n - 1)]
         pltpu.make_async_copy(part, part, send_g.at[base]).wait()
 
     pl.semaphore_wait(barrier, n - 1)
@@ -434,39 +440,50 @@
     def flag_of(i):
         return edge.block(i)[0] if i < ex else 3 + edge.pattern_of[i - ex]
 
-    def build_edges(f, field):
-        for t in range(tiles):
-            acc = None
+    def build_edges(f, field, group):
+        moved = {}
+        for t in group:
             for j in range(edge.places):
                 slab = edge.slab(t, j)
-                start = GROUP * j
                 if slab is None:
-                    acc = jnp.where(lane >= start, 0.0, acc)
-                    break
+                    continue
                 s, side = slab
                 which, k = edge.block(s)
-                at = 2 * HALO * k
+                start, at = GROUP * j, 2 * HALO * k
                 if side == 0:
                     own = spin(field[s], start + HALO)
                     far = spin(z_in[f, 1, which], start - at)
-                    here = jnp.where(lane < start + HALO, far, own)
                 else:
                     own = spin(field[s], start + 2 * HALO - bz)
                     far = spin(z_in[f, 0, which], start + HALO - at)
+                moved[t, j] = own, far
+        yield
+        for t in group:
+            acc = None
+            for j in range(edge.places):
+                start = GROUP * j
+                if (t, j) not in moved:
+                    acc = jnp.where(lane >= start, 0.0, acc)
+                    break
+                own, far = moved[t, j]
+                if edge.slab(t, j)[1] == 0:
+                    here = jnp.where(lane < start + HALO, far, own)
+                else:
                     here = jnp.where(lane < start + 2 * HALO, own, far)
                 acc = here if acc is None else jnp.where(lane >= start, here, acc)
             field[ex + t] = jnp.where(lane < GROUP * edge.places, acc, 0.0)
 
-    def pool_yz(v):
-        v = v + jnp.where(odd_row, up_y(v), dn_y(v))
-        return v + jnp.where(odd_lane, up_z(v), dn_z(v))
-
-    def groups(lo, hi):
+    def pair_y(v):
+        rows = v.reshape(ey // 8, 8, bz)
+        swapped = jnp.where(odd_row, pltpu.roll(rows, 1, 1), pltpu.roll(rows, 7, 1))
+        return (rows + swapped).reshape(ey, bz)
+
+    def groups(lo, hi, span=SPAN):
         out = []
         for a, b in ((lo, hi), (ex, ex + tiles)):
             at = a
             while at < b:
-                stop = min(b, at + SPAN - (at - a) % SPAN)
+                stop = min(b, at + span)
                 out.append(list(range(at, stop)))
                 at = stop
         return out
@@ -522,6 +539,8 @@
                 except StopIteration:
                     done |= gives
             open_items = still
+            if not open_items and at < len(items):
+                assert items[at][1] <= done, items[at][1] - done
             if at < len(items) and items[at][1] <= done:
                 gen, _, gives = items[at]
                 at += 1
@@ -543,33 +562,129 @@
         FL[k] = (z_f < a).astype(f32)
         F1[k] = (even_f < a).astype(f32)
 
-    build_edges(1, C)
-    every = list(range(ex)) + list(range(ex, ex + tiles))
-    for i in every:
-        c = C[i]
-        if i != 0:
-            before = spin(C[ex + tiles - 1], GROUP) if i == ex else C[i - 1]
-            FX[i] = 0.5 * (before + c)
-        FY[i] = 0.5 * (c + up_y(c))
-        FZ[i] = 0.5 * (c + up_z(c))
-    FX[ex + tiles] = spin(FX[ex], -GROUP)
-    for i in list(range(1, ex - 1)) + list(range(ex, ex + tiles)):
-        fy, fz = FY[i], FZ[i]
-        diagonal = (FX[i] + FX[i + 1]) + (fy + dn_y(fy)) + (fz + dn_z(fz))
-        fl = FL[flag_of(i)]
-        INV[i] = OMEGA * fl / (diagonal + 1.0 - fl)
+    items = []
     pairs, edge_pairs = ex // 2, tiles // 2
-    for q in range(pairs + edge_pairs):
-        C1[q] = pool_yz(C[2 * q] + C[2 * q + 1]) * 0.125
-    for q in list(range(1, pairs - 1)) + list(range(pairs, pairs + edge_pairs)):
-        c = C1[q]
-        before = spin(C1[pairs + edge_pairs - 1], GROUP) if q == pairs else C1[q - 1]
-        after = spin(C1[pairs], -GROUP) if q == pairs + edge_pairs - 1 else C1[q + 1]
-        diagonal = 3.0 * c + 0.5 * (
-            (before + after) + (up_y(c, 2) + dn_y(c, 2)) + (up_z(c, 2) + dn_z(c, 2))
-        )
-        fl = F1[flag_of(2 * q)]
-        IC[q] = OMEGA * fl / (4.0 * diagonal + 1.0 - fl)
+    last_pair = pairs + edge_pairs - 1
+
+    def make_faces(group):
+        up = {i: up_z(C[i]) for i in group}
+        (b, kb), _ = around(group[0])
+        before = None if group[0] == 0 else spin(C[b], kb)
+        yield
+        for i in group:
+            c = C[i]
+            if before is not None:
+                FX[i] = 0.5 * (before + c)
+            before = c
+            FY[i] = 0.5 * (c + up_y(c))
+            FZ[i] = 0.5 * (c + up[i])
+
+    def make_wrap():
+        around_face = spin(FX[ex], -GROUP)
+        yield
+        FX[ex + tiles] = around_face
+
+    def make_inverse(group):
+        dn = {i: dn_z(FZ[i]) for i in group}
+        yield
+        for i in group:
+            fy = FY[i]
+            diagonal = (FX[i] + FX[i + 1]) + (fy + dn_y(fy)) + (FZ[i] + dn[i])
+            fl = FL[flag_of(i)]
+            INV[i] = OMEGA * fl / (diagonal + 1.0 - fl)
+
+    def make_pooled(group):
+        pooled = {}
+        for q in group:
+            v = pair_y(C[2 * q] + C[2 * q + 1])
+            pooled[q] = v, up_z(v), dn_z(v)
+        yield
+        for q in group:
+            v, up, dn = pooled[q]
+            C1[q] = (v + jnp.where(odd_lane, up, dn)) * 0.125
+
+    def beside(q):
+        before = (last_pair, GROUP) if q == pairs else (q - 1, 0)
+        after = (pairs, -GROUP) if q == last_pair else (q + 1, 0)
+        return before, after
+
+    def make_coarse_inverse(group):
+        found = {}
+        for q in group:
+            c = C1[q]
+            (b, kb), (a, ka) = beside(q)
+            found[q] = up_z(c, 2), dn_z(c, 2), spin(C1[b], kb), spin(C1[a], ka)
+        yield
+        for q in group:
+            c = C1[q]
+            up, dn, before, after = found[q]
+            diagonal = 3.0 * c + 0.5 * ((before + after) + (up_y(c, 2) + dn_y(c, 2)) + (up + dn))
+            fl = F1[flag_of(2 * q)]
+            IC[q] = OMEGA * fl / (4.0 * diagonal + 1.0 - fl)
+
+    def cut(lo, hi, span):
+        return [list(range(a, min(hi, a + span))) for a in range(lo, hi, span)]
+
+    def named(name, these):
+        return {(name, i) for i in these}
+
+    def face_items(lo, hi, needs):
+        return [
+            (make_faces(g), needs if lo < ex else named("c", range(tiles)), named("f", g))
+            for g in cut(lo, hi, WIDE)
+        ]
+
+    def inverse_items(lo, hi):
+        return [
+            (make_inverse(g), named("f", g + [g[-1] + 1]), named("i", g)) for g in cut(lo, hi, WIDE)
+        ]
+
+    def pooled_items(lo, hi):
+        needs = set() if lo < pairs else named("c", range(tiles))
+        return [(make_pooled(g), needs, named("p", g)) for g in cut(lo, hi, WIDE // 2)]
+
+    def coarse_items(lo, hi):
+        return [
+            (
+                make_coarse_inverse(g),
+                named("p", [at for q in g for at, _ in beside(q)] + g),
+                named("n", g),
+            )
+            for g in cut(lo, hi, WIDE // 2)
+        ]
+
+    def edge_items(f, name):
+        field = (R, C)[f]
+        return [
+            (build_edges(f, field, g), set() if f else {"arrived"}, named(name, g))
+            for g in cut(0, tiles, EDGES)
+        ]
+
+    def mixed(*lists):
+        out, lists = [], [list(x) for x in lists]
+        while any(lists):
+            for x in lists:
+                if x:
+                    out.append(x.pop(0))
+        return out
+
+    def arrive():
+        wait_all(0)
+        yield
+
+    items += mixed(
+        edge_items(1, "c"),
+        face_items(0, ex, set()) + inverse_items(1, ex - 1),
+        pooled_items(0, pairs) + coarse_items(1, pairs - 1),
+    )
+    items.append((arrive(), set(), {"arrived"}))
+    items += mixed(
+        edge_items(0, "r"),
+        face_items(ex, ex + tiles, None)
+        + [(make_wrap(), named("f", [ex]), named("f", [ex + tiles]))]
+        + inverse_items(ex, ex + tiles),
+        pooled_items(pairs, pairs + edge_pairs) + coarse_items(pairs, pairs + edge_pairs),
+    )
 
     off = lane_y % GROUP
     slot0 = (lane_y // GROUP) * tiles
@@ -641,8 +756,6 @@
         late_row = late_row + jnp.where(col == base + me, diagonal, 0.0)
         coupling[0] = late_row
 
-    wait_all(0)
-    build_edges(0, R)
 
     def solve(means):
         y_row = jnp.sum(inverse * means, axis=0, keepdims=True)
@@ -662,10 +775,11 @@
             EY[k] = FL[k] * v
 
     cells = bx * by * bz
-    collect(early, 0)
-    m0_col = early[:, 0, 0:1]
 
     def first_solve():
+        collect(early, 0)
+        m0_col = early[:, 0, 0:1]
+        yield
         y_row = jnp.sum(inverse * (m0_col * (1.0 / cells)), axis=0, keepdims=True)
         yield
         y_col = jnp.sum(jnp.where(eye, y_row, 0.0), axis=1, keepdims=True)
@@ -673,7 +787,7 @@
         yield
         spread_blocks(y_col)
 
-    items = [(first_solve(), set(), {"blocks"})]
+    items.append((first_solve(), set(), {"blocks"}))
     sums = [[zeros, zeros] for _ in range(7)]
     parts = {}
 
@@ -690,7 +804,7 @@
         for i in group[::2]:
             gap = FL[flag_of(i)] * (field[i] - found[i][1])
             gap = gap + FL[flag_of(i + 1)] * (field[i + 1] - found[i + 1][1])
-            gap = gap + jnp.where(odd_row, up_y(gap), dn_y(gap))
+            gap = pair_y(gap)
             pooled[i] = (gap, up_z(gap), dn_z(gap))
         yield
         for i in group[::2]:
@@ -713,7 +827,12 @@
     def add_cycle(field, source, name, lo, hi, keep, extra):
         even, stop = (lo - 1) // 2 * 2, (hi + 2) // 2 * 2
         for group in groups(even, stop):
-            needs = set() if source is None else reads(source, group)
+            if source is None:
+                needs = {(k, at) for k in "fi" for _, at in reads("i", group)}
+                needs |= named("n", [i // 2 for i in group]) | {"arrived"}
+                needs |= named("r", range(tiles)) if group[0] >= ex else set()
+            else:
+                needs = reads(source, group)
             items.append((coarse(field, group), needs, {(name + "s", i) for i in group}))
         for group in groups(lo, hi):
             needs = reads(name + "s", group) | extra
@@ -768,6 +887,7 @@
     late_row = coupling[0]
     for k in range(7):
         late_row = jnp.where(col == k, parts[k], late_row)
+    late_row = jnp.where(col == 7, m0, late_row)
     late_out[...] = late_row
     late[pl.ds(me, 1)] = late_row[None]
     spread(late_out, late, 1)
@@ -785,9 +905,8 @@
         return jnp.sum(line[:, k : k + 1], axis=(0, 1), keepdims=True)
 
     rz, dad = pick(plain, 0), pick(plain, 1)
-    y_m0 = total(m0_col * y_col)
     w_u = pick(plain, 3) + pick(weighted, 2)
-    r_u = pick(plain, 4) + y_m0
+    r_u = pick(plain, 4) + pick(weighted, 7)
     u_q = (
         pick(plain, 5)
         + 2.0 * pick(weighted, 6)
@@ -826,6 +945,8 @@
             ref[x] = jnp.where(
                 lane_y < HALO, low, jnp.where(lane_y >= bz - HALO, high, ref[x])
             )
+    spread_done(early, 0)
+    spread_done(late, 1)
 
 
 def solution(mesh):

time: 23.4 us -> 23.1 us (0.987)
  no operation moved by 1% of the time
where the time goes in v4:
time: 23.1 us; the launch traced here: 23 us
  Pallas kernels  21 us (91%)
  between operations  1.28 us (6%)
  local copies, waits for them, and re-layouts  0.66 us (3%)
    pallas_call x1, Pallas kernels, on_device(): pl.pallas_call(functools.partial(kernel, counts), out_shape=vm(2, bx, by,...  21 us
    squeeze x1, local copies, waits for them, and re-layouts, on_device(): return (both[0], both[1])  0.66 us

profile of v4, /device:TPU:0, one launch (start us, length us, event | category | flops | bytes accessed | tf_op | source)
XLA Modules:
  0.0 23.0 jit_solution(4520587839112105790)
XLA Ops:
  1.3 21.0 %shard_map.59 = f32[2,8,16,128]{3,2,1,0:T(8,128)S(1)} custom-call(f32[8,16,128]{2,1,0:T(8,128)} %rhs_hbm.1, f32[8,16,128]{2,1,0:T(8,128)} %cond_hbm.1, s32[1,1,1]{2,1,0:T(1,128)S(6)} %copy.6.ext_hbm, bf16[32,32]{1,0:T(8,128)(2,1)} %factor_hbm.1), custom_call_target="tpu_custom_call" | custom-call | tf_op jit(solution)/shard_map/pallas_call | solution.py:1008
  22.3 0.7 %slice_bitcast_fusion = (f32[8,16,128]{2,1,0:T(8,128)}, f32[8,16,128]{2,1,0:T(8,128)}) fusion(f32[2,8,16,128]{3,2,1,0:T(8,128)S(1)} %shard_map.59), kind=kLoop, calls=%fused_computation | loop fusion | bytes 262144 | tf_op jit(solution)/shard_map/squeeze | solution.py:1018

commit v5 on v4

--- a/solution.py
+++ b/solution.py
@@ -787,7 +787,6 @@
         yield
         spread_blocks(y_col)
 
-    items.append((first_solve(), set(), {"blocks"}))
     sums = [[zeros, zeros] for _ in range(7)]
     parts = {}
 
@@ -835,15 +834,20 @@
                 needs = reads(source, group)
             items.append((coarse(field, group), needs, {(name + "s", i) for i in group}))
         for group in groups(lo, hi):
-            needs = reads(name + "s", group) | extra
+            needs = reads(name + "s", group)
+            if extra and group[0] >= ex:
+                items.append(extra)
+                extra = None
             items.append((smooth(field, group, keep), needs, {(name, i) for i in group}))
 
     def keep_direction(i, v):
-        D0[i] = v + EY[flag_of(i)]
+        U[i] = v
 
     def keep_image(i, v, lv):
         w = FL[flag_of(i)] * lv
         W[i] = w
+        if lo_x <= i < hi_x or i >= ex:
+            D0[i] = v
         add(i, 0, R[i, :by] * v[:by])
         add(i, 1, w[:by] * v[:by])
         add(i, 2, w[:by])
@@ -868,12 +872,12 @@
     def core_of(name):
         return {(name, i) for i in range(lo_x, hi_x)} | {(name, ex + t) for t in range(tiles)}
 
-    add_cycle(R, None, "d", 4, ex - 4, keep_direction, {"blocks"})
+    add_cycle(R, None, "d", 4, ex - 4, keep_direction, (first_solve(), set(), {"blocks"}))
     for group in groups(5, ex - 5):
         items.append(
-            (image(lambda i: D0[i], group, keep_image), reads("d", group), {("w", i) for i in group})
+            (image(lambda i: U[i] + EY[flag_of(i)], group, keep_image), reads("d", group) | {"blocks"}, {("w", i) for i in group})
         )
-    add_cycle(W, "w", "u", 7, ex - 7, keep_second, set())
+    add_cycle(W, "w", "u", 7, ex - 7, keep_second, None)
     items.append((couple(), set(), set()))
     items.append((gather_sums(range(3)), core_of("w"), set()))
     for group in groups(lo_x, hi_x):
@@ -888,18 +892,39 @@
     for k in range(7):
         late_row = jnp.where(col == k, parts[k], late_row)
     late_row = jnp.where(col == 7, m0, late_row)
+    compact = base + 2 * n <= width
+    if compact:
+        late_row = jnp.where(col == base + n + me, parts[2], late_row)
     late_out[...] = late_row
     late[pl.ds(me, 1)] = late_row[None]
     spread(late_out, late, 1)
+    if compact:
+        spot = lax.broadcasted_iota(jnp.int32, (n, width), 1)
+        owner = lax.broadcasted_iota(jnp.int32, (n, width), 0)
+        own_lane = spot == base + owner
+        placed = jnp.dot(
+            inverse,
+            (spot == base + n + owner).astype(f32),
+            precision=HIGH,
+            preferred_element_type=f32,
+        )
     wait_sent(1)
     wait_sent(0)
     collect(late, 1)
 
     rows = late[:, 0, :]
-    y_row, y_col = solve(rows[:, 2:3] * (1.0 / cells))
+    plain = jnp.sum(rows, axis=0, keepdims=True)
+    if compact:
+        y_col = jnp.sum(placed * plain, axis=1, keepdims=True) * (1.0 / cells)
+    else:
+        y_row, y_col = solve(rows[:, 2:3] * (1.0 / cells))
     spread_blocks(y_col)
-    plain = jnp.sum(rows, axis=0, keepdims=True)
     weighted = jnp.sum(rows * y_col, axis=0, keepdims=True)
+    if compact:
+        y_line = jnp.sum(jnp.where(own_lane, y_col, 0.0), axis=0, keepdims=True)
+        quadratic = total(weighted * y_line)
+    else:
+        quadratic = total(weighted[:, base : base + n] * y_row)
 
     def pick(line, k):
         return jnp.sum(line[:, k : k + 1], axis=(0, 1), keepdims=True)
@@ -910,11 +935,11 @@
     u_q = (
         pick(plain, 5)
         + 2.0 * pick(weighted, 6)
-        + total(weighted[:, base : base + n] * y_row)
+        + quadratic
     )
-    alpha = rz / dad
+    alpha, per_rz = rz / dad, 1.0 / rz
     new = (rz - alpha * dad) + alpha * (alpha * w_u - r_u)
-    beta = new / rz
+    beta = new * per_rz
     grow = 1.0 + beta
     dad1 = grow * grow * dad - 2.0 * alpha * grow * w_u + alpha * alpha * u_q
     alpha1 = new / dad1

time: 23.1 us -> 23 us (level)
  no operation moved by 1% of the time
where the time goes in v5:
time: 23 us; the launch traced here: 22.9 us
  Pallas kernels  20.9 us (91%)
  between operations  1.28 us (6%)
  local copies, waits for them, and re-layouts  0.66 us (3%)
    pallas_call x1, Pallas kernels, on_device(): pl.pallas_call(functools.partial(kernel, counts), out_shape=vm(2, bx, by,...  20.9 us
    squeeze x1, local copies, waits for them, and re-layouts, on_device(): return (both[0], both[1])  0.66 us

profile of v5, /device:TPU:0, one launch (start us, length us, event | category | flops | bytes accessed | tf_op | source)
XLA Modules:
  0.0 22.9 jit_solution(17901828042751996101)
XLA Ops:
  1.3 20.9 %shard_map.59 = f32[2,8,16,128]{3,2,1,0:T(8,128)S(1)} custom-call(f32[8,16,128]{2,1,0:T(8,128)} %rhs_hbm.1, f32[8,16,128]{2,1,0:T(8,128)} %cond_hbm.1, s32[1,1,1]{2,1,0:T(1,128)S(6)} %copy.6.ext_hbm, bf16[32,32]{1,0:T(8,128)(2,1)} %factor_hbm.1), custom_call_target="tpu_custom_call" | custom-call | tf_op jit(solution)/shard_map/pallas_call | solution.py:1033
  22.2 0.7 %slice_bitcast_fusion = (f32[8,16,128]{2,1,0:T(8,128)}, f32[8,16,128]{2,1,0:T(8,128)}) fusion(f32[2,8,16,128]{3,2,1,0:T(8,128)S(1)} %shard_map.59), kind=kLoop, calls=%fused_computation | loop fusion | bytes 262144 | tf_op jit(solution)/shard_map/squeeze | solution.py:1043

commit v6 on v5

--- a/solution.py
+++ b/solution.py
@@ -448,6 +448,9 @@
                 if slab is None:
                     continue
                 s, side = slab
+                if f == 0 and s in (0, ex - 1):
+                    moved[t, j] = None
+                    continue
                 which, k = edge.block(s)
                 start, at = GROUP * j, 2 * HALO * k
                 if side == 0:
@@ -465,7 +468,7 @@
                 if (t, j) not in moved:
                     acc = jnp.where(lane >= start, 0.0, acc)
                     break
-                own, far = moved[t, j]
+                own, far = moved[t, j] or (0.0, 0.0)
                 if edge.slab(t, j)[1] == 0:
                     here = jnp.where(lane < start + HALO, far, own)
                 else:
@@ -951,25 +954,37 @@
         sol = c1 * D0[i, :by] - c2 * (U[i, :by] + v[:by])
         res = fl * R[i, :by] - c1 * W[i, :by] + c2 * (Q[i, :by] + fl * lv[:by])
         if i < ex:
-            sol_ref[i - lo_x], res_ref[i - lo_x] = sol, res
+            inner[i - lo_x] = sol, res
         else:
             SEC[i, :by], INV[i, :by] = sol, res
 
-    run(
-        [
-            (image(lambda i: EY[flag_of(i)], group, results), set(), set())
-            for group in groups(lo_x, hi_x)
-        ]
-    )
-    for x in range(bx):
-        tl, jl = edge.place(lo_x + x, 0)
-        th, jh = edge.place(lo_x + x, 1)
-        for ref, held in ((sol_ref, SEC), (res_ref, INV)):
-            low = spin(held[ex + tl, :by], -(GROUP * jl + HALO))
-            high = spin(held[ex + th, :by], bz - HALO - (GROUP * jh + HALO))
-            ref[x] = jnp.where(
-                lane_y < HALO, low, jnp.where(lane_y >= bz - HALO, high, ref[x])
-            )
+    inner = {}
+
+    def turn_edges(xs):
+        ends = {}
+        for x in xs:
+            tl, jl = edge.place(lo_x + x, 0)
+            th, jh = edge.place(lo_x + x, 1)
+            ends[x] = [
+                (
+                    spin(held[ex + tl, :by], -(GROUP * jl + HALO)),
+                    spin(held[ex + th, :by], bz - HALO - (GROUP * jh + HALO)),
+                )
+                for held in (SEC, INV)
+            ]
+        yield
+        for x in xs:
+            for ref, whole, (low, high) in zip((sol_ref, res_ref), inner[x], ends[x]):
+                whole = jnp.where(lane_y >= bz - HALO, high, whole)
+                ref[x] = jnp.where(lane_y < HALO, low, whole)
+
+    steps = [
+        (image(lambda i: EY[flag_of(i)], group, results), set(), named("out", group))
+        for group in reversed(groups(lo_x, hi_x))
+    ]
+    around_x = named("out", list(range(lo_x, hi_x)) + list(range(ex, ex + tiles)))
+    steps += [(turn_edges(xs), around_x, set()) for xs in cut(0, bx, bx // 2)]
+    run(steps)
     spread_done(early, 0)
     spread_done(late, 1)
 

time: 23 us -> 23 us (level)
  no operation moved by 1% of the time
where the time goes in v6:
time: 23 us; the launch traced here: 22.8 us
  Pallas kernels  20.9 us (91%)
  between operations  1.28 us (6%)
  local copies, waits for them, and re-layouts  0.66 us (3%)
    pallas_call x1, Pallas kernels, on_device(): pl.pallas_call(functools.partial(kernel, counts), out_shape=vm(2, bx, by,...  20.9 us
    squeeze x1, local copies, waits for them, and re-layouts, on_device(): return (both[0], both[1])  0.66 us

profile of v6, /device:TPU:0, one launch (start us, length us, event | category | flops | bytes accessed | tf_op | source)
XLA Modules:
  0.0 22.8 jit_solution(8312283914419710752)
XLA Ops:
  1.3 20.9 %shard_map.59 = f32[2,8,16,128]{3,2,1,0:T(8,128)S(1)} custom-call(f32[8,16,128]{2,1,0:T(8,128)} %rhs_hbm.1, f32[8,16,128]{2,1,0:T(8,128)} %cond_hbm.1, s32[1,1,1]{2,1,0:T(1,128)S(6)} %copy.6.ext_hbm, bf16[32,32]{1,0:T(8,128)(2,1)} %factor_hbm.1), custom_call_target="tpu_custom_call" | custom-call | tf_op jit(solution)/shard_map/pallas_call | solution.py:1048
  22.2 0.7 %slice_bitcast_fusion = (f32[8,16,128]{2,1,0:T(8,128)}, f32[8,16,128]{2,1,0:T(8,128)}) fusion(f32[2,8,16,128]{3,2,1,0:T(8,128)S(1)} %shard_map.59), kind=kLoop, calls=%fused_computation | loop fusion | bytes 262144 | tf_op jit(solution)/shard_map/squeeze | solution.py:1058

commit v7 on v6

--- a/solution.py
+++ b/solution.py
@@ -378,6 +378,7 @@
             preferred_element_type=f32,
         )
         s *= 2
+    relay(1)
     inverse = lax.dot_general(
         X, X, (((0,), (0,)), ((), ())), precision=HIGH, preferred_element_type=f32
     )
@@ -553,7 +554,6 @@
                 except StopIteration:
                     done |= gives
 
-    relay(1)
     wait_all(1)
     relay(0)
 

time: 23 us -> 23 us (level)
  no operation moved by 1% of the time
where the time goes in v7:
time: 23 us; the launch traced here: 22.8 us
  Pallas kernels  20.9 us (91%)
  between operations  1.28 us (6%)
  local copies, waits for them, and re-layouts  0.66 us (3%)
    pallas_call x1, Pallas kernels, on_device(): pl.pallas_call(functools.partial(kernel, counts), out_shape=vm(2, bx, by,...  20.9 us
    squeeze x1, local copies, waits for them, and re-layouts, on_device(): return (both[0], both[1])  0.66 us

profile of v7, /device:TPU:0, one launch (start us, length us, event | category | flops | bytes accessed | tf_op | source)
XLA Modules:
  0.0 22.8 jit_solution(18424168616752097518)
XLA Ops:
  1.3 20.9 %shard_map.59 = f32[2,8,16,128]{3,2,1,0:T(8,128)S(1)} custom-call(f32[8,16,128]{2,1,0:T(8,128)} %rhs_hbm.1, f32[8,16,128]{2,1,0:T(8,128)} %cond_hbm.1, s32[1,1,1]{2,1,0:T(1,128)S(6)} %copy.6.ext_hbm, bf16[32,32]{1,0:T(8,128)(2,1)} %factor_hbm.1), custom_call_target="tpu_custom_call" | custom-call | tf_op jit(solution)/shard_map/pallas_call | solution.py:1048
  22.2 0.7 %slice_bitcast_fusion = (f32[8,16,128]{2,1,0:T(8,128)}, f32[8,16,128]{2,1,0:T(8,128)}) fusion(f32[2,8,16,128]{3,2,1,0:T(8,128)S(1)} %shard_map.59), kind=kLoop, calls=%fused_computation | loop fusion | bytes 262144 | tf_op jit(solution)/shard_map/squeeze | solution.py:1058
